TPU v7x, 128 devices: a whole 4x4x4 slice. The times are simulated.
128 devices in a mesh: gx: 8 (over z, core), yz: 16 (over y, x).
Axes of the slice: x: 4, y: 4, z: 4, core: 2. Of those that a mesh axis runs over, the one named last changes fastest.
Arguments:
- brick_ids: int32 [16384, 1], P(('gx', 'yz')), may hold values from 0 to 127; in each aligned block of 128 rows (0 to 127, 128 to 255, ...) at most 2 rows name the same one
- voxel_offset: int32 [16384, 256], P(('gx', 'yz')), may hold values from 0 to 4095
- fractions: float32 [16384, 3, 256], P(('gx', 'yz')), may hold values from 0 to 1
- normals: float32 [16384, 3, 256], P(('gx', 'yz')), may hold values from -6 to 6
- point_weight: float32 [16384, 256], P(('gx', 'yz')), may hold values from 0.1 to 10
- tile_count: int32 [128], P(('gx', 'yz')), may hold values from 96 to 128, as said below
Outputs:
- rhs: float32 [32, 128, 128], P('gx', 'yz')
- screen: float32 [32, 128, 128], P('gx', 'yz')
Inputs may be any that keep to these rules, and one draw needn't show every extreme that they name: `brick_ids`: brick b belongs to index b // 16 of gx and b % 16 of yz. Among the 128 tile slots of one device no brick is named more than 2 times. `tile_count`: some device has all its slots valid in every draw.
All inputs are finite; a program needn't handle non-finite values.
Results may differ from a plain program's by a relative error of at most 0.0039.
Values sent between devices are 32-bit elements; how exact they have to be, the bound alone decides.
A program may use at most 64 MiB of HBM per device.

v0:
```python
import jax
import jax.numpy as jnp
from jax import lax
from jax.sharding import PartitionSpec as P

BX = 4
BY = 8
BZ = 128


def passed_along(value, axis, steps):
    count = lax.axis_size(axis)
    first, last = (max(0, -steps), min(count, count - steps))
    return lax.ppermute(value, axis, [(source, source + steps) for source in range(first, last)])


def spline(frac):
    weights = [0.5 * (1.0 - frac) ** 2, 0.75 - (frac - 0.5) ** 2, 0.5 * frac * frac]
    slopes = [frac - 1.0, 1.0 - 2.0 * frac, frac]
    return (weights, slopes)


def splat_block(carry, points):
    rhs_acc, screen_acc = carry
    channels = jnp.transpose(points, (1, 0, 2)).reshape(8, -1)
    offset = channels[0].astype(jnp.int32)
    cell_x = offset // (BY * BZ)
    cell_y = offset // BZ % BY
    cell_z = offset % BZ
    wx, gx = spline(channels[1])
    wy, gy = spline(channels[2])
    wz, gz = spline(channels[3])
    nx = channels[4]
    ny = channels[5]
    nz = channels[6]
    weight = channels[7]
    plane_rows = jnp.arange((BX + 2) * (BY + 2), dtype=jnp.int32)[:, None]
    depth_cols = jnp.arange(BZ, dtype=jnp.int32)[None, :]
    count = offset.shape[0]
    a_twelve = jnp.zeros(((BX + 2) * (BY + 2), count), jnp.float32)
    a_three = jnp.zeros_like(a_twelve)
    a_screen = jnp.zeros_like(a_twelve)
    for first in range(3):
        for second in range(3):
            target = ((cell_x + first) * (BY + 2) + cell_y + second)[None, :]
            hit = plane_rows == target
            term_twelve = nx * gx[first] * wy[second] + ny * wx[first] * gy[second]
            term_three = nz * wx[first] * wy[second]
            term_screen = weight * wx[first] * wy[second]
            a_twelve = a_twelve + jnp.where(hit, term_twelve[None, :], 0.0)
            a_three = a_three + jnp.where(hit, term_three[None, :], 0.0)
            a_screen = a_screen + jnp.where(hit, term_screen[None, :], 0.0)
    z_value = jnp.zeros((count, BZ), jnp.float32)
    z_slope = jnp.zeros_like(z_value)
    for third in range(3):
        hit = (cell_z + third - 1)[:, None] == depth_cols
        z_value = z_value + jnp.where(hit, wz[third][:, None], 0.0)
        z_slope = z_slope + jnp.where(hit, gz[third][:, None], 0.0)
    z_value = z_value.astype(jnp.bfloat16)
    left = jnp.concatenate([a_twelve, a_three], axis=1).astype(jnp.bfloat16)
    right = jnp.concatenate([z_value, z_slope.astype(jnp.bfloat16)], axis=0)
    rhs_acc = rhs_acc + jnp.dot(left, right, preferred_element_type=jnp.float32)
    screen_acc = screen_acc + jnp.dot(
        a_screen.astype(jnp.bfloat16), z_value, preferred_element_type=jnp.float32
    )
    return ((rhs_acc, screen_acc), None)


def shards(brick_ids, voxel_offset, fractions, normals, point_weight, tile_count):
    n_slabs = lax.axis_size("gx")
    n_columns = lax.axis_size("yz")
    devices = n_slabs * n_columns
    tiles_here = brick_ids.shape[0]
    tile_len = voxel_offset.shape[1]
    capacity = max(2, (tiles_here + devices - 1) // devices)
    dest = brick_ids[:, 0]
    order = jnp.arange(tiles_here, dtype=jnp.int32)
    valid = order < tile_count[0]
    earlier = (dest[:, None] == dest[None, :]) & valid[None, :] & (order[None, :] < order[:, None])
    rank = jnp.sum(earlier.astype(jnp.int32), axis=1)
    slots = devices * capacity
    target = jnp.where(valid, dest * capacity + rank, slots)
    packed = jnp.concatenate(
        [
            voxel_offset.astype(jnp.float32)[:, None, :],
            fractions,
            normals,
            point_weight[:, None, :],
        ],
        axis=1,
    )
    outbox = jnp.zeros((slots, 8, tile_len), jnp.float32).at[target].set(packed, mode="drop")
    inbox = lax.all_to_all(outbox, ("gx", "yz"), split_axis=0, concat_axis=0, tiled=True)
    group = 16
    blocks = inbox.reshape(slots // group, group, 8, tile_len)
    plane = (BX + 2) * (BY + 2)
    start = (jnp.zeros((plane, BZ), jnp.float32), jnp.zeros((plane, BZ), jnp.float32))
    (rhs_acc, screen_acc), _ = lax.scan(splat_block, start, blocks)
    field = jnp.stack([rhs_acc, screen_acc]).reshape(2, BX + 2, BY + 2, BZ)
    from_below = passed_along(field[:, BX + 1], "gx", 1)
    from_above = passed_along(field[:, 0], "gx", -1)
    field = field.at[:, 1].add(from_below)
    field = field.at[:, BX].add(from_above)
    inner = field[:, 1 : BX + 1]
    from_left = passed_along(inner[:, :, BY + 1], "yz", 1)
    from_right = passed_along(inner[:, :, 0], "yz", -1)
    inner = inner.at[:, :, 1].add(from_left)
    inner = inner.at[:, :, BY].add(from_right)
    result = inner[:, :, 1 : BY + 1]
    return (result[0], result[1])


def solution(mesh):
    return jax.shard_map(
        shards,
        mesh=mesh,
        in_specs=(
            P(("gx", "yz"), None),
            P(("gx", "yz"), None),
            P(("gx", "yz"), None, None),
            P(("gx", "yz"), None, None),
            P(("gx", "yz"), None),
            P(("gx", "yz")),
        ),
        out_specs=(P("gx", "yz", None), P("gx", "yz", None)),
        check_vma=False,
    )
```

profile of v0, /device:TPU:0, one launch (start us, length us, event | category | flops | bytes accessed | tf_op | source)
XLA Modules:
  0.0 264.5 jit_solution(6114821710073582594)
XLA Ops:
  5.8 13.6 %scatter_fusion = f32[256,8,256]{2,1,0:T(8,128)} fusion(f32[256,8,256]{2,1,0:T(8,128)} %broadcast_in_dim.553, s32[128]{0:T(128)S(1)} %fusion.71, f32[128,8,256]{2,1,0:T(8,128)S(1)} %copy.17), kind=kCustom, calls=%fused_computation | custom fusion | bytes 3146240 | tf_op jit(solution)/shard_map/scatter | solution.py:92
  19.5 11.1 %all-to-all-start = ((f32[256,8,256]{2,1,0:T(8,128)}), f32[256,8,256]{2,1,0:T(8,128)S(1)}, u32[]{:S(2)}, u32[]{:S(2)}) async-start(f32[256,8,256]{2,1,0:T(8,128)} %scatter_fusion), calls=%async_computation | async-start | bytes 4194304 | tf_op jit(solution)/shard_map/all_to_all | solution.py:93
  30.6 29.8 %all-to-all-done = f32[256,8,256]{2,1,0:T(8,128)S(1)} async-done(((f32[256,8,256]{2,1,0:T(8,128)}), f32[256,8,256]{2,1,0:T(8,128)S(1)}, u32[]{:S(2)}, u32[]{:S(2)}) %all-to-all-start) | async-done | bytes 2097184 | tf_op jit(solution)/shard_map/all_to_all | solution.py:93
  60.4 188.6 %while.22 = (s32[]{:T(128)}, f32[60,128]{1,0:T(8,128)S(1)}, f32[60,128]{1,0:T(8,128)S(1)}, f32[16,16,8,256]{3,2,1,0:T(8,128)S(1)}, s32[]{:T(128)}, /*index=5*/s32[]{:T(128)}) while((s32[]{:T(128)}, f32[60,128]{1,0:T(8,128)S(1)}, f32[60,128]{1,0:T(8,128)S(1)}, f32[16,16,8,256]{3,2,1,0:T(8,128)S(1)}, s32[]{:T(128)}, ...), condition=%wide.region_3.4_spmd.clone, body=%wide.region_2.3_spmd.clone.sunk | while | flops 228026368 | bytes 8839260 | solution.py:98
  60.7 3.6 %convolution_add_fusion.2 = f32[60,128]{1,0:T(8,128)S(1)} fusion(f32[4096]{0:T(1024)S(1)} %get-tuple-element.440, f32[4096]{0:T(1024)S(1)} %get-tuple-element.441, f32[4096]{0:T(1024)S(1)} %get-tuple-element.442, f32[4096]{0:T(1024)S(1)} %get-tuple-element.443, f32[4096]{0:T(1024)S(1)} %get-tuple-element.444, f32[4096]{0:T(1024)S(1)} %get-tuple-element.445, ...), kind=kOutput, calls=%fused_computation.11.clone.1 | convolution fusion | flops 74284032 | bytes 454657 | tf_op jit(solution)/shard_map/while/body/eval_jaxpr/dot_general | solution.py:63
  66.1 5.5 %add_convert_fusion.14 = (bf16[4096,128]{1,0:T(8,128)(2,1)S(1)}, bf16[4096,128]{1,0:T(8,128)(2,1)S(1)}) fusion(f32[4096]{0:T(1024)S(1)} %get-tuple-element.403, s32[4096]{0:T(1024)S(1)} %get-tuple-element.405, f32[4096]{0:T(1024)S(1)} %get-tuple-element.406, s32[4096]{0:T(1024)S(1)} %get-tuple-element.407, f32[4096]{0:T(1024)S(1)} %get-tuple-element.408, ...), kind=kLoop, calls=%fused_computation.6.clone.2 | loop fusion | flops 7864320 | bytes 2244608 | tf_op jit(solution)/shard_map/while/body/eval_jaxpr/convert_element_type | solution.py:59
  72.5 3.6 %convolution_add_fusion.2 = f32[60,128]{1,0:T(8,128)S(1)} fusion(f32[4096]{0:T(1024)S(1)} %get-tuple-element.440, f32[4096]{0:T(1024)S(1)} %get-tuple-element.441, f32[4096]{0:T(1024)S(1)} %get-tuple-element.442, f32[4096]{0:T(1024)S(1)} %get-tuple-element.443, f32[4096]{0:T(1024)S(1)} %get-tuple-element.444, f32[4096]{0:T(1024)S(1)} %get-tuple-element.445, ...), kind=kOutput, calls=%fused_computation.11.clone.1 | convolution fusion | flops 74284032 | bytes 454657 | tf_op jit(solution)/shard_map/while/body/eval_jaxpr/dot_general | solution.py:63
  77.9 5.5 %add_convert_fusion.14 = (bf16[4096,128]{1,0:T(8,128)(2,1)S(1)}, bf16[4096,128]{1,0:T(8,128)(2,1)S(1)}) fusion(f32[4096]{0:T(1024)S(1)} %get-tuple-element.403, s32[4096]{0:T(1024)S(1)} %get-tuple-element.405, f32[4096]{0:T(1024)S(1)} %get-tuple-element.406, s32[4096]{0:T(1024)S(1)} %get-tuple-element.407, f32[4096]{0:T(1024)S(1)} %get-tuple-element.408, ...), kind=kLoop, calls=%fused_computation.6.clone.2 | loop fusion | flops 7864320 | bytes 2244608 | tf_op jit(solution)/shard_map/while/body/eval_jaxpr/convert_element_type | solution.py:59
  89.7 5.5 %add_convert_fusion.14 = (bf16[4096,128]{1,0:T(8,128)(2,1)S(1)}, bf16[4096,128]{1,0:T(8,128)(2,1)S(1)}) fusion(f32[4096]{0:T(1024)S(1)} %get-tuple-element.403, s32[4096]{0:T(1024)S(1)} %get-tuple-element.405, f32[4096]{0:T(1024)S(1)} %get-tuple-element.406, s32[4096]{0:T(1024)S(1)} %get-tuple-element.407, f32[4096]{0:T(1024)S(1)} %get-tuple-element.408, ...), kind=kLoop, calls=%fused_computation.6.clone.2 | loop fusion | flops 7864320 | bytes 2244608 | tf_op jit(solution)/shard_map/while/body/eval_jaxpr/convert_element_type | solution.py:59
  96.0 3.6 %convolution_add_fusion.2 = f32[60,128]{1,0:T(8,128)S(1)} fusion(f32[4096]{0:T(1024)S(1)} %get-tuple-element.440, f32[4096]{0:T(1024)S(1)} %get-tuple-element.441, f32[4096]{0:T(1024)S(1)} %get-tuple-element.442, f32[4096]{0:T(1024)S(1)} %get-tuple-element.443, f32[4096]{0:T(1024)S(1)} %get-tuple-element.444, f32[4096]{0:T(1024)S(1)} %get-tuple-element.445, ...), kind=kOutput, calls=%fused_computation.11.clone.1 | convolution fusion | flops 74284032 | bytes 454657 | tf_op jit(solution)/shard_map/while/body/eval_jaxpr/dot_general | solution.py:63
  101.5 5.5 %add_convert_fusion.14 = (bf16[4096,128]{1,0:T(8,128)(2,1)S(1)}, bf16[4096,128]{1,0:T(8,128)(2,1)S(1)}) fusion(f32[4096]{0:T(1024)S(1)} %get-tuple-element.403, s32[4096]{0:T(1024)S(1)} %get-tuple-element.405, f32[4096]{0:T(1024)S(1)} %get-tuple-element.406, s32[4096]{0:T(1024)S(1)} %get-tuple-element.407, f32[4096]{0:T(1024)S(1)} %get-tuple-element.408, ...), kind=kLoop, calls=%fused_computation.6.clone.2 | loop fusion | flops 7864320 | bytes 2244608 | tf_op jit(solution)/shard_map/while/body/eval_jaxpr/convert_element_type | solution.py:59
  113.3 5.5 %add_convert_fusion.14 = (bf16[4096,128]{1,0:T(8,128)(2,1)S(1)}, bf16[4096,128]{1,0:T(8,128)(2,1)S(1)}) fusion(f32[4096]{0:T(1024)S(1)} %get-tuple-element.403, s32[4096]{0:T(1024)S(1)} %get-tuple-element.405, f32[4096]{0:T(1024)S(1)} %get-tuple-element.406, s32[4096]{0:T(1024)S(1)} %get-tuple-element.407, f32[4096]{0:T(1024)S(1)} %get-tuple-element.408, ...), kind=kLoop, calls=%fused_computation.6.clone.2 | loop fusion | flops 7864320 | bytes 2244608 | tf_op jit(solution)/shard_map/while/body/eval_jaxpr/convert_element_type | solution.py:59
  125.1 5.5 %add_convert_fusion.14 = (bf16[4096,128]{1,0:T(8,128)(2,1)S(1)}, bf16[4096,128]{1,0:T(8,128)(2,1)S(1)}) fusion(f32[4096]{0:T(1024)S(1)} %get-tuple-element.403, s32[4096]{0:T(1024)S(1)} %get-tuple-element.405, f32[4096]{0:T(1024)S(1)} %get-tuple-element.406, s32[4096]{0:T(1024)S(1)} %get-tuple-element.407, f32[4096]{0:T(1024)S(1)} %get-tuple-element.408, ...), kind=kLoop, calls=%fused_computation.6.clone.2 | loop fusion | flops 7864320 | bytes 2244608 | tf_op jit(solution)/shard_map/while/body/eval_jaxpr/convert_element_type | solution.py:59
  136.9 5.5 %add_convert_fusion.14 = (bf16[4096,128]{1,0:T(8,128)(2,1)S(1)}, bf16[4096,128]{1,0:T(8,128)(2,1)S(1)}) fusion(f32[4096]{0:T(1024)S(1)} %get-tuple-element.403, s32[4096]{0:T(1024)S(1)} %get-tuple-element.405, f32[4096]{0:T(1024)S(1)} %get-tuple-element.406, s32[4096]{0:T(1024)S(1)} %get-tuple-element.407, f32[4096]{0:T(1024)S(1)} %get-tuple-element.408, ...), kind=kLoop, calls=%fused_computation.6.clone.2 | loop fusion | flops 7864320 | bytes 2244608 | tf_op jit(solution)/shard_map/while/body/eval_jaxpr/convert_element_type | solution.py:59
  148.7 5.5 %add_convert_fusion.14 = (bf16[4096,128]{1,0:T(8,128)(2,1)S(1)}, bf16[4096,128]{1,0:T(8,128)(2,1)S(1)}) fusion(f32[4096]{0:T(1024)S(1)} %get-tuple-element.403, s32[4096]{0:T(1024)S(1)} %get-tuple-element.405, f32[4096]{0:T(1024)S(1)} %get-tuple-element.406, s32[4096]{0:T(1024)S(1)} %get-tuple-element.407, f32[4096]{0:T(1024)S(1)} %get-tuple-element.408, ...), kind=kLoop, calls=%fused_computation.6.clone.2 | loop fusion | flops 7864320 | bytes 2244608 | tf_op jit(solution)/shard_map/while/body/eval_jaxpr/convert_element_type | solution.py:59
  160.4 5.5 %add_convert_fusion.14 = (bf16[4096,128]{1,0:T(8,128)(2,1)S(1)}, bf16[4096,128]{1,0:T(8,128)(2,1)S(1)}) fusion(f32[4096]{0:T(1024)S(1)} %get-tuple-element.403, s32[4096]{0:T(1024)S(1)} %get-tuple-element.405, f32[4096]{0:T(1024)S(1)} %get-tuple-element.406, s32[4096]{0:T(1024)S(1)} %get-tuple-element.407, f32[4096]{0:T(1024)S(1)} %get-tuple-element.408, ...), kind=kLoop, calls=%fused_computation.6.clone.2 | loop fusion | flops 7864320 | bytes 2244608 | tf_op jit(solution)/shard_map/while/body/eval_jaxpr/convert_element_type | solution.py:59
  172.2 5.5 %add_convert_fusion.14 = (bf16[4096,128]{1,0:T(8,128)(2,1)S(1)}, bf16[4096,128]{1,0:T(8,128)(2,1)S(1)}) fusion(f32[4096]{0:T(1024)S(1)} %get-tuple-element.403, s32[4096]{0:T(1024)S(1)} %get-tuple-element.405, f32[4096]{0:T(1024)S(1)} %get-tuple-element.406, s32[4096]{0:T(1024)S(1)} %get-tuple-element.407, f32[4096]{0:T(1024)S(1)} %get-tuple-element.408, ...), kind=kLoop, calls=%fused_computation.6.clone.2 | loop fusion | flops 7864320 | bytes 2244608 | tf_op jit(solution)/shard_map/while/body/eval_jaxpr/convert_element_type | solution.py:59
  184.0 5.5 %add_convert_fusion.14 = (bf16[4096,128]{1,0:T(8,128)(2,1)S(1)}, bf16[4096,128]{1,0:T(8,128)(2,1)S(1)}) fusion(f32[4096]{0:T(1024)S(1)} %get-tuple-element.403, s32[4096]{0:T(1024)S(1)} %get-tuple-element.405, f32[4096]{0:T(1024)S(1)} %get-tuple-element.406, s32[4096]{0:T(1024)S(1)} %get-tuple-element.407, f32[4096]{0:T(1024)S(1)} %get-tuple-element.408, ...), kind=kLoop, calls=%fused_computation.6.clone.2 | loop fusion | flops 7864320 | bytes 2244608 | tf_op jit(solution)/shard_map/while/body/eval_jaxpr/convert_element_type | solution.py:59
  195.8 5.5 %add_convert_fusion.14 = (bf16[4096,128]{1,0:T(8,128)(2,1)S(1)}, bf16[4096,128]{1,0:T(8,128)(2,1)S(1)}) fusion(f32[4096]{0:T(1024)S(1)} %get-tuple-element.403, s32[4096]{0:T(1024)S(1)} %get-tuple-element.405, f32[4096]{0:T(1024)S(1)} %get-tuple-element.406, s32[4096]{0:T(1024)S(1)} %get-tuple-element.407, f32[4096]{0:T(1024)S(1)} %get-tuple-element.408, ...), kind=kLoop, calls=%fused_computation.6.clone.2 | loop fusion | flops 7864320 | bytes 2244608 | tf_op jit(solution)/shard_map/while/body/eval_jaxpr/convert_element_type | solution.py:59
  207.6 5.5 %add_convert_fusion.14 = (bf16[4096,128]{1,0:T(8,128)(2,1)S(1)}, bf16[4096,128]{1,0:T(8,128)(2,1)S(1)}) fusion(f32[4096]{0:T(1024)S(1)} %get-tuple-element.403, s32[4096]{0:T(1024)S(1)} %get-tuple-element.405, f32[4096]{0:T(1024)S(1)} %get-tuple-element.406, s32[4096]{0:T(1024)S(1)} %get-tuple-element.407, f32[4096]{0:T(1024)S(1)} %get-tuple-element.408, ...), kind=kLoop, calls=%fused_computation.6.clone.2 | loop fusion | flops 7864320 | bytes 2244608 | tf_op jit(solution)/shard_map/while/body/eval_jaxpr/convert_element_type | solution.py:59
  219.4 5.5 %add_convert_fusion.14 = (bf16[4096,128]{1,0:T(8,128)(2,1)S(1)}, bf16[4096,128]{1,0:T(8,128)(2,1)S(1)}) fusion(f32[4096]{0:T(1024)S(1)} %get-tuple-element.403, s32[4096]{0:T(1024)S(1)} %get-tuple-element.405, f32[4096]{0:T(1024)S(1)} %get-tuple-element.406, s32[4096]{0:T(1024)S(1)} %get-tuple-element.407, f32[4096]{0:T(1024)S(1)} %get-tuple-element.408, ...), kind=kLoop, calls=%fused_computation.6.clone.2 | loop fusion | flops 7864320 | bytes 2244608 | tf_op jit(solution)/shard_map/while/body/eval_jaxpr/convert_element_type | solution.py:59
  231.2 5.5 %add_convert_fusion.14 = (bf16[4096,128]{1,0:T(8,128)(2,1)S(1)}, bf16[4096,128]{1,0:T(8,128)(2,1)S(1)}) fusion(f32[4096]{0:T(1024)S(1)} %get-tuple-element.403, s32[4096]{0:T(1024)S(1)} %get-tuple-element.405, f32[4096]{0:T(1024)S(1)} %get-tuple-element.406, s32[4096]{0:T(1024)S(1)} %get-tuple-element.407, f32[4096]{0:T(1024)S(1)} %get-tuple-element.408, ...), kind=kLoop, calls=%fused_computation.6.clone.2 | loop fusion | flops 7864320 | bytes 2244608 | tf_op jit(solution)/shard_map/while/body/eval_jaxpr/convert_element_type | solution.py:59
  243.0 5.5 %add_convert_fusion.14 = (bf16[4096,128]{1,0:T(8,128)(2,1)S(1)}, bf16[4096,128]{1,0:T(8,128)(2,1)S(1)}) fusion(f32[4096]{0:T(1024)S(1)} %get-tuple-element.403, s32[4096]{0:T(1024)S(1)} %get-tuple-element.405, f32[4096]{0:T(1024)S(1)} %get-tuple-element.406, s32[4096]{0:T(1024)S(1)} %get-tuple-element.407, f32[4096]{0:T(1024)S(1)} %get-tuple-element.408, ...), kind=kLoop, calls=%fused_computation.6.clone.2 | loop fusion | flops 7864320 | bytes 2244608 | tf_op jit(solution)/shard_map/while/body/eval_jaxpr/convert_element_type | solution.py:59
  259.7 4.1 %collective-permute-done.3 = f32[2,4,128]{2,1,0:T(4,128)S(1)} collective-permute-done((f32[2,4,128]{2,1,0:T(4,128)S(1)}, f32[2,4,128]{2,1,0:T(4,128)S(1)}, u32[]{:S(2)}, u32[]{:S(2)}) %collective-permute-start.3) | collective-permute-done | bytes 4128 | tf_op jit(solution)/shard_map/ppermute | solution.py:14
  (192 shorter events, 103.7 us)
Async XLA Ops:
  2.2 1.9 copy-start
  19.5 40.9 %all-to-all-start = ((f32[256,8,256]{2,1,0:T(8,128)}), f32[256,8,256]{2,1,0:T(8,128)S(1)}, u32[]{:S(2)}, u32[]{:S(2)}) async-start(f32[256,8,256]{2,1,0:T(8,128)} %scatter_fusion), calls=%async_computation | async-start | bytes 4194304 | tf_op jit(solution)/shard_map/all_to_all | solution.py:93
  249.1 2.1 collective-permute-start
  251.2 4.1 %collective-permute-start.1 = (f32[2,10,128]{2,0,1:T(2,128)S(1)}, f32[2,10,128]{2,0,1:T(2,128)S(1)}, u32[]{:S(2)}, u32[]{:S(2)}) collective-permute-start(f32[2,10,128]{2,0,1:T(2,128)S(1)} %get-tuple-element.316), channel_id=1, source_target_pairs={{16,0},{32,16},{48,32},{64,48},{80,64},{96,80},{112,96},{17,1},{33... | collective-permute-start | bytes 30728 | tf_op jit(solution)/shard_map/ppermute | solution.py:14
  255.4 4.2 %collective-permute-start.2 = (f32[2,4,128]{2,1,0:T(4,128)S(1)}, f32[2,4,128]{2,1,0:T(4,128)S(1)}, u32[]{:S(2)}, u32[]{:S(2)}) collective-permute-start(f32[2,4,128]{2,1,0:T(4,128)S(1)} %get-tuple-element.313), channel_id=1, source_target_pairs={{0,1},{1,2},{2,3},{3,4},{4,5},{5,6},{6,7},{7,8},{8,9},{9,10},{10,1... | collective-permute-start | bytes 12296 | tf_op jit(solution)/shard_map/ppermute | solution.py:14
  258.3 5.5 %collective-permute-start.3 = (f32[2,4,128]{2,1,0:T(4,128)S(1)}, f32[2,4,128]{2,1,0:T(4,128)S(1)}, u32[]{:S(2)}, u32[]{:S(2)}) collective-permute-start(f32[2,4,128]{2,1,0:T(4,128)S(1)} %get-tuple-element.312), channel_id=1, source_target_pairs={{1,0},{2,1},{3,2},{4,3},{5,4},{6,5},{7,6},{8,7},{9,8},{10,9},{11,1... | collective-permute-start | bytes 12296 | tf_op jit(solution)/shard_map/ppermute | solution.py:14
where the time goes:
time: 269 us; the launch traced here: 264 us
  other arithmetic  124 us (46%)
  matrix products  65.9 us (24%)
  waiting for transfers between devices  37.4 us (14%)
  starting transfers between devices  17.9 us (7%)
  local copies, waits for them, and re-layouts  16.8 us (6%)
    convert_element_type x16, other arithmetic, splat_block(): z_value = z_value.astype(jnp.bfloat16)  88.3 us
    dot_general x16, matrix products, splat_block(): jnp.dot(a_screen.astype(jnp.bfloat16), z_value, preferred_element_type=jn...  58 us
    all_to_all x1, waiting for transfers between devices, shards(): lax.all_to_all(outbox, ('gx', 'yz'), split_axis=0, concat_axis=0, tiled=T...  29.8 us
    another operation x32, other arithmetic  29.1 us
    scatter x1, local copies, waits for them, and re-layouts, shards(): jnp.zeros((slots, 8, tile_len), jnp.float32).at[target]  13.6 us
    all_to_all x1, starting transfers between devices, shards(): lax.all_to_all(outbox, ('gx', 'yz'), split_axis=0, concat_axis=0, tiled=T...  11.1 us
    dot_general x16, matrix products, splat_block(): rhs_acc = rhs_acc + jnp.dot(left, right, preferred_element_type=jnp.float32)  7.87 us
    ppermute x4, waiting for transfers between devices, passed_along(): lax.ppermute(value, axis, [(source, source + steps) for source in range(f...  7.67 us
  transfers between devices with their start and end apart: 5, of which 4 were waited for; matrix products, arithmetic and copies ran while one was open for 0% of the time, Pallas kernels for 0%

commit v1 on v0

v1 whole, which is shorter than its diff:
```python
import jax
import jax.numpy as jnp
from jax import lax
from jax.experimental import pallas as pl
from jax.experimental.pallas import tpu as pltpu
from jax.sharding import PartitionSpec as P

BX, BY, BZ = 4, 8, 128
PX, PY = 36, 152
U = 8

CZ0, CZ1, CZ2, WZ0, WZ1, WZ2, GZ0, GZ1, GZ2 = range(9)
CX, WX0, WX1, WX2, GX0, GX1, GX2 = range(9, 16)
CY, WY0, WY1, WY2, GY0, GY1, GY2 = range(16, 23)
QNX, QNY, QNZ, QS = range(23, 27)
NQ = 27


def spline(f):
    return ((0.5 * (1.0 - f) ** 2, 0.75 - (f - 0.5) ** 2, 0.5 * f * f),
            (f - 1.0, 1.0 - 2.0 * f, f))


def prepare(count, off_ref, frac_ref, norm_ref, s_ref, q_ref):
    tiles = off_ref.shape[0]

    def put(k, r, value):
        for h in range(2):
            q_ref[k, h, r, :] = value[:, h * 128:h * 128 + 128]

    def group(g, _):
        r = pl.ds(pl.multiple_of(g * 8, 8), 8)
        off = off_ref[r, :]
        row = g * 8 + lax.broadcasted_iota(jnp.int32, off.shape, 0)
        valid = (row < count).astype(jnp.float32)
        cz = (off & (BZ - 1)).astype(jnp.float32)
        put(CZ0, r, cz - 1.0)
        put(CZ1, r, cz)
        put(CZ2, r, cz + 1.0)
        put(CX, r, (off >> 10).astype(jnp.float32))
        put(CY, r, ((off >> 7) & (BY - 1)).astype(jnp.float32))
        for dim, w0, g0 in ((0, WX0, GX0), (1, WY0, GY0), (2, WZ0, GZ0)):
            w, s = spline(frac_ref[dim, r, :])
            for k in range(3):
                put(w0 + k, r, w[k])
                put(g0 + k, r, s[k])
        for k in range(3):
            put(QNX + k, r, norm_ref[k, r, :] * valid)
        put(QS, r, s_ref[r, :] * valid)
        return 0

    lax.fori_loop(0, tiles // 8, group, 0)


def ROW(q_ref, k, h, t):
    return q_ref[k, h, pl.ds(t, 8, stride=0), :]


def bc(row, n=8):
    return jnp.broadcast_to(row, (n, row.shape[1]))


def tile_build(t, q_ref):
    parts = [half_build(t, h, q_ref) for h in range(2)]
    return tuple(jnp.concatenate(p, 1) for p in zip(*parts))


def half_build(t, h, q_ref):
    def row(k):
        return ROW(q_ref, k, h, t)

    def half(k):
        r = row(k)
        return jnp.concatenate([r, r], 0).astype(jnp.bfloat16)

    n = 128
    lanes = (8, n)
    cz = [half(CZ0 + k) for k in range(3)]
    wz = [half(WZ0 + k) for k in range(3)]
    gz = [half(GZ0 + k) for k in range(3)]
    zero = jnp.zeros((16, n), jnp.bfloat16)
    zb, zd = [], []
    for i in range(BZ // 16):
        at = (lax.broadcasted_iota(jnp.int32, (16, n), 0) + 16 * i).astype(jnp.bfloat16)
        hit = [at == c for c in cz]
        zb.append(jnp.where(hit[0], wz[0], jnp.where(hit[1], wz[1], jnp.where(hit[2], wz[2], zero))))
        zd.append(jnp.where(hit[0], gz[0], jnp.where(hit[1], gz[1], jnp.where(hit[2], gz[2], zero))))
    zb = jnp.concatenate(zb, 0)
    zd = jnp.concatenate(zd, 0)

    at = lax.broadcasted_iota(jnp.int32, lanes, 0).astype(jnp.float32)
    zf = jnp.zeros(lanes, jnp.float32)

    def spread(c, w0, g0):
        hit = [at == c + float(k) for k in range(3)]
        out = []
        for base in (w0, g0):
            v = [row(base + k) for k in range(3)]
            out.append(jnp.where(hit[0], v[0], jnp.where(hit[1], v[1], jnp.where(hit[2], v[2], zf))))
        return out

    wx, gx = spread(row(CX), WX0, GX0)
    cy = row(CY)
    wy, gy = spread(cy, WY0, GY0)
    last, before = cy == float(BY - 1), cy == float(BY - 2)
    wy8 = jnp.where(last, row(WY1), jnp.where(before, row(WY2), zf))
    gy8 = jnp.where(last, row(GY1), jnp.where(before, row(GY2), zf))
    wy9 = jnp.where(last, row(WY2), zf)
    gy9 = jnp.where(last, row(GY2), zf)
    p12x = row(QNX) * gx
    p12y = row(QNY) * wx
    p3 = row(QNZ) * wx
    ps = row(QS) * wx
    a12, a3, a_s = [], [], []
    for x in range(BX + 2):
        r = slice(x, x + 1)
        a12.append(bc(p12x[r]) * wy + bc(p12y[r]) * gy)
        a3.append(bc(p3[r]) * wy)
        a_s.append(bc(ps[r]) * wy)
    for w, g in ((wy8, gy8), (wy9, gy9)):
        a12.append(p12x * w + p12y * g)
        a3.append(p3 * w)
        a_s.append(ps * w)
    lhs1 = jnp.concatenate(a12 + a_s, 0).astype(jnp.bfloat16)
    lhs2 = jnp.concatenate(a3, 0).astype(jnp.bfloat16)
    return lhs1, lhs2, zb, zd


def contract(lhs1, lhs2, zb, zd):
    nt = (((1,), (1,)), ((), ()))
    r1 = lax.dot_general(lhs1, zb, nt, preferred_element_type=jnp.float32)
    r2 = lax.dot_general(lhs2, zd, nt, preferred_element_type=jnp.float32)
    return r1[:64] + r2, r1[64:]


def add_in(b, res, out_ref):
    x0 = (b // 16) * BX
    y0 = (b % 16) * BY + 7
    for f in range(2):
        base = (f * PX + x0) * PY + y0
        for x in range(BX + 2):
            r = pl.ds(base + x * PY, 8)
            out_ref[r, :] += res[f][8 * x:8 * x + 8]
        for k in range(2):
            r = pl.ds(base + 8 + k, 8, stride=PY)
            out_ref[r, :] += res[f][48 + 8 * k:56 + 8 * k]


def splat_kernel(dest_ref, count_ref, off_ref, frac_ref, norm_ref, s_ref, out_ref, q_ref):
    count = count_ref[0]
    out_ref[...] = jnp.zeros_like(out_ref)
    prepare(count, off_ref, frac_ref, norm_ref, s_ref, q_ref)

    def body(i, _):
        ts = [i * U + u for u in range(U)]
        res = [contract(*tile_build(t, q_ref)) for t in ts]
        for t, r in zip(ts, res):
            add_in(dest_ref[t], r, out_ref)
        return 0

    lax.fori_loop(0, (count + U - 1) // U, body, 0)


def splat(dest, count, off, frac, norm, s):
    tiles, n = off.shape
    vm = pl.BlockSpec(memory_space=pltpu.VMEM)
    sm = pl.BlockSpec(memory_space=pltpu.SMEM)
    return pl.pallas_call(
        splat_kernel,
        out_shape=jax.ShapeDtypeStruct((2 * PX * PY, BZ), jnp.float32),
        in_specs=[sm, sm, vm, vm, vm, vm],
        out_specs=vm,
        scratch_shapes=[pltpu.VMEM((NQ, 2, tiles, 128), jnp.float32)],
        compiler_params=pltpu.CompilerParams(vmem_limit_bytes=40 << 20),
        name="splat",
    )(dest, count, off, jnp.transpose(frac, (1, 0, 2)), jnp.transpose(norm, (1, 0, 2)), s)


def shards(brick_ids, voxel_offset, fractions, normals, point_weight, tile_count):
    grid = splat(brick_ids[:, 0], tile_count, voxel_offset, fractions, normals, point_weight)
    slabs, columns = lax.axis_size("gx"), lax.axis_size("yz")
    grid = grid.reshape(2, PX, PY, BZ)[:, 1:1 + slabs * BX, BY:BY + columns * BY]
    chunks = grid.reshape(2, slabs, BX, columns, BY, BZ).transpose(1, 3, 0, 2, 4, 5)
    chunks = chunks.reshape(slabs * columns, 2, BX, BY, BZ)
    mine = lax.psum_scatter(chunks, ("gx", "yz"), scatter_dimension=0, tiled=True)[0]
    return mine[0], mine[1]


def solution(mesh):
    return jax.shard_map(
        shards,
        mesh=mesh,
        in_specs=(
            P(("gx", "yz"), None),
            P(("gx", "yz"), None),
            P(("gx", "yz"), None, None),
            P(("gx", "yz"), None, None),
            P(("gx", "yz"), None),
            P(("gx", "yz")),
        ),
        out_specs=(P("gx", "yz", None), P("gx", "yz", None)),
        check_vma=False,
    )
```

time: 269 us -> 690 us (2.57)
  waiting for transfers between devices: 37.4 us -> 655 us
  other arithmetic: 124 us -> 0 us
  matrix products: 65.9 us -> 0 us
  starting transfers between devices: 17.9 us -> 0.04 us
  between operations: 1.49 us -> 14.7 us
  Pallas kernels: 0 us -> 10.6 us
  local copies, waits for them, and re-layouts: 16.8 us -> 8.88 us
    reduce_scatter x0 -> x1, waiting for transfers between devices: none -> 655 us  [shards(): lax.psum_scatter(chunks, ('gx', 'yz'), scatter_dimension=0, tiled=True)[0]]
    convert_element_type x16 -> x0, other arithmetic: 88.3 us -> none  [splat_block(): z_value = z_value.astype(jnp.bfloat16)]
    dot_general x32 -> x0, matrix products: 65.9 us -> none  [the longest x16 58 us: splat_block(): jnp.dot(a_screen.astype(jnp.bfloat16), z_value, preferred_element_type=jn...]
    all_to_all x1 -> x0, waiting for transfers between devices: 29.8 us -> none  [shards(): lax.all_to_all(outbox, ('gx', 'yz'), split_axis=0, concat_axis=0, tiled=T...]
    another operation x33 -> x0, other arithmetic: 29.1 us -> none
    scatter x1 -> x0, local copies, waits for them, and re-layouts: 13.6 us -> none  [shards(): jnp.zeros((slots, 8, tile_len), jnp.float32).at[target]]
    all_to_all x1 -> x0, starting transfers between devices: 11.1 us -> none  [shards(): lax.all_to_all(outbox, ('gx', 'yz'), split_axis=0, concat_axis=0, tiled=T...]
    pallas_call x0 -> x1, Pallas kernels: none -> 10.6 us  [splat(): pl.pallas_call(splat_kernel, out_shape=jax.ShapeDtypeStruct((2 * PX * PY,...]
  transfers between devices with their start and end apart: 5 -> 1, of which waited for: 4 -> 1; matrix products, arithmetic and copies ran while one was open for 0% -> 0% of each run, Pallas kernels for 0% -> 0%
where the time goes in v1:
time: 690 us; the launch traced here: 689 us
  waiting for transfers between devices  655 us (95%)
  between operations  14.7 us (2%)
  Pallas kernels  10.6 us (2%)
  local copies, waits for them, and re-layouts  8.88 us (1%)
    reduce_scatter x1, waiting for transfers between devices, shards(): lax.psum_scatter(chunks, ('gx', 'yz'), scatter_dimension=0, tiled=True)[0]  655 us
  transfers between devices with their start and end apart: 1, of which 1 were waited for; matrix products, arithmetic and copies ran while one was open for 0% of the time, Pallas kernels for 0%

profile of v1, /device:TPU:0, one launch (start us, length us, event | category | flops | bytes accessed | tf_op | source)
XLA Modules:
  0.0 689.4 jit_solution(7495157033034336278)
XLA Ops:
  7.2 0.0 reduce-scatter.2.cloned.1.call-start
  7.9 0.0 copy-start
  7.9 1.0 copy-done
  8.9 0.0 copy-start.1
  8.9 1.0 copy-done.1
  9.8 0.0 copy-start.2
  9.9 0.9 copy-done.2
  10.8 0.0 copy-start.3
  10.8 0.9 copy-done.3
  11.7 0.0 copy-start.4
  11.7 0.7 copy-done.4
  12.3 10.6 %splat.1 = f32[10944,128]{1,0:T(8,128)S(1)} custom-call(s32[128]{0:T(128)S(1)} %bitcast.15, s32[1]{0:T(128)S(6)} %copy.9.count_ref, s32[128,256]{1,0:T(8,128)S(1)} %copy-done.2, f32[3,128,256]{2,1,0:T(8,128)S(1)} %bitcast.13, f32[3,128,256]{2,1,0:T(8,128)S(1)} %bitcast.14, f32[128,256]{1,0:T(8,128)S(1)} %copy-done.3), custom_call_target="tpu_custom_call" | custom-call | tf_op jit(solution)/shard_map/splat/pallas_call | solution.py:168
  22.9 0.5 slice.14
  23.4 2.5 copy.8
  26.0 0.0 reduce-scatter.2.cloned.1.call-update
  26.0 655.2 %reduce-scatter.2.cloned.1.call-done = f32[1,2,4,8,128]{4,3,2,1,0:T(8,128)} async-done(((f32[128,2,4,8,128]{4,3,2,1,0:T(8,128)}), f32[1,2,4,8,128]{4,3,2,1,0:T(8,128)}) %reduce-scatter.2.cloned.1.call-update) | async-done | bytes 32784 | tf_op jit(solution)/shard_map/reduce_scatter | solution.py:185
  681.2 1.3 slice_bitcast_fusion
Async XLA Ops:
  7.2 674.1 %reduce-scatter.2.cloned.1.call-start = ((), (), s32[]{:S(2)}) async-start(), calls=%async_computation.1 | async-start | bytes 4227072 | tf_op jit(solution)/shard_map/reduce_scatter | solution.py:185
  7.9 1.0 copy-start
  8.9 1.0 copy-start.1
  9.8 0.9 copy-start.2
  10.8 0.9 copy-start.3
  11.7 0.7 copy-start.4
Sparse Core Ops, SparseCore 0:
  26.1 655.0 reduce-scatter.1

commit v2 on v1

--- a/solution.py
+++ b/solution.py
@@ -176,14 +176,201 @@
     )(dest, count, off, jnp.transpose(frac, (1, 0, 2)), jnp.transpose(norm, (1, 0, 2)), s)
 
 
+N = 4
+MESH = pl.DeviceIdType.MESH
+
+
+class Copies:
+    def __init__(self, send_sems, recv_sems):
+        self.send_sems, self.recv_sems = send_sems, recv_sems
+        self.made = []
+
+    def start(self, src, dst, device):
+        i = len(self.made)
+        copy = pltpu.make_async_remote_copy(
+            src_ref=src, dst_ref=dst, send_sem=self.send_sems.at[i], recv_sem=self.recv_sems.at[i],
+            device_id=device, device_id_type=MESH)
+        copy.start()
+        self.made.append(copy)
+        return copy
+
+    def finish(self):
+        for copy in self.made:
+            copy.wait_send()
+
+
+def reduce_kernel(grid_ref, rhs_ref, screen_ref, pair_ref, sum_ref, xa, xb, xc, xr, ya, yb, yc, yr, za, zb, zc, zr,
+                  sx, sy, sz, rx, ry, rz, send_sems, recv_sems, ready_sem):
+    slab, column = lax.axis_index("gx"), lax.axis_index("yz")
+    pz, core = slab // 2, slab % 2
+    py, px = column // N, column % N
+
+    def device(dz=0, dy=0, dx=0):
+        return (((pz + dz) % N) * 2 + core, ((py + dy) % N) * N + (px + dx) % N)
+
+    other = (pz * 2 + 1 - core, column)
+    lines = [device(**{axis: k}) for axis in ("dz", "dy", "dx") for k in range(1, N)]
+
+    barrier = pltpu.get_barrier_semaphore()
+    for peer in [other] + lines:
+        pl.semaphore_signal(barrier, inc=1, device_id=peer, device_id_type=MESH)
+    pl.semaphore_wait(barrier, 1 + len(lines))
+
+    copies = Copies(send_sems, recv_sems)
+
+    def slab_rows(j, which):
+        return pl.ds(1 + BX * (((pz + j) % N) * 2 + which), BX)
+
+    order = (2, 1, 3, 0)
+    pair = {}
+    for j in order:
+        pair[j] = copies.start(grid_ref.at[:, slab_rows(j, 1 - core), pl.ds(BY, 128), :], pair_ref.at[j], other)
+    for peer in lines:
+        pl.semaphore_signal(ready_sem, inc=1, device_id=peer, device_id_type=MESH)
+
+    def data_x(j, h, d):
+        return (j, slice(0, 3), slice(2 * h, 2 * h + 2), (px + d) % N)
+
+    def data_y(j, h, d):
+        return (j, slice(3, 6), (py + d) % N, slice(2 * h, 2 * h + 2))
+
+    def data_z(j, h, d):
+        return (d % N, 6 + h)
+
+    parts = {"x": (data_x, "dx", xa, xb, xc, xr), "y": (data_y, "dy", ya, yb, yc, yr), "z": (data_z, "dz", za, zb, zc, zr)}
+    first, second, third = {}, {}, {}
+
+    def toward(name, way):
+        return device(**{parts[name][1]: 1 if way == 0 else N - 1})
+
+    def send_far(name, j):
+        data, _, a, _, _, _ = parts[name]
+        for way in range(2):
+            first[name, j, way] = copies.start(sum_ref.at[data(j, way, 2)], a.at[j, way], toward(name, way))
+
+    def send_near(name, j, ways=(0, 1)):
+        data, _, _, b, _, _ = parts[name]
+        for way in ways:
+            second[name, j, way] = copies.start(sum_ref.at[data(j, 1 - way, 1 if way == 0 else N - 1)], b.at[j, way],
+                                                toward(name, way))
+
+    def relay(name, j):
+        data, _, a, _, c, r = parts[name]
+        for way in range(2):
+            first[name, j, way].wait_recv()
+            r[j, way] = a[j, way] + sum_ref[data(j, way, 1 if way == 0 else N - 1)]
+            third[name, j, way] = copies.start(r.at[j, way], c.at[j, way], toward(name, way))
+
+    for at, j in enumerate(order):
+        pair[j].wait_recv()
+        rows = 1 + BX * (((pz + j) % N) * 2 + core)
+        for f in range(2):
+            def add_plane(x, _, f=f, rows=rows, j=j):
+                total = grid_ref[f, rows + x, pl.ds(BY, 128), :] + pair_ref[j, f, x]
+                sum_ref[j, BX * f + x] = total.reshape(N, N, BY, BZ)
+                return 0
+            lax.fori_loop(0, BX, add_plane, 0)
+        send_far("x", j)
+        send_far("y", j)
+        if j == 2:
+            send_far("z", 0)
+        send_near("x", j)
+        send_near("y", j)
+        if j == 1:
+            send_near("z", 0, (0,))
+        if j == 3:
+            send_near("z", 0, (1,))
+        if at >= 2:
+            relay("x", order[at - 2])
+            relay("y", order[at - 2])
+        if at == 2:
+            relay("z", 0)
+    for j in order[2:]:
+        relay("x", j)
+        relay("y", j)
+
+    pl.semaphore_wait(ready_sem, len(lines))
+
+    def joined(name, j, own):
+        _, _, _, b, c, _ = parts[name]
+        for way in range(2):
+            second[name, j, way].wait_recv()
+            third[name, j, way].wait_recv()
+        return [own(h) + c[j, h] + b[j, 1 - h] for h in range(2)]
+
+    last = []
+    for j in order:
+        for name, data, s, r in (("x", data_x, sx, rx), ("y", data_y, sy, ry)):
+            low, high = joined(name, j, lambda h: sum_ref[data(j, h, 0)])
+            s[j, :, 0:2] = low
+            s[j, :, 2:4] = high
+            for m in (2, 1, 3, 0):
+                if (j, m) == (0, 0):
+                    continue
+                if name == "x":
+                    where = s.at[j, :, (py + m) % N]
+                    peer = device(dz=j, dy=m)
+                else:
+                    where = s.at[j, :, (px + m) % N]
+                    peer = device(dz=j, dx=m)
+                last.append(copies.start(where, r.at[j, m], peer))
+    low, high = joined("z", 0, lambda h: sum_ref[data_z(0, h, 0)])
+    sz[0] = low
+    sz[1] = high
+    for j in order:
+        for m in (2, 1, 3, 0):
+            if (j, m) == (0, 0):
+                continue
+            last.append(copies.start(sz.at[:, (py + j) % N, (px + m) % N], rz.at[j, m], device(dy=j, dx=m)))
+    for copy in last:
+        copy.wait_recv()
+
+    others = [(j, m) for j in range(N) for m in range(N) if (j, m) != (0, 0)]
+
+    def total(own, r):
+        for j, m in others:
+            own = own + r[j, m]
+        return own
+
+    fx = total(sx[0, :, py], rx)
+    fy = total(sy[0, :, px], ry)
+    fz = total(sz[:, py, px], rz)
+    rhs_ref[0:3] = fx
+    rhs_ref[3] = fy[0]
+    screen_ref[0:2] = fy[1:3]
+    screen_ref[2:4] = fz
+    copies.finish()
+
+
+def reduce_grid(grid):
+    vm = pl.BlockSpec(memory_space=pltpu.VMEM)
+    f32 = jnp.float32
+    half = pltpu.VMEM((N, 2, 3, 2, BY, BZ), f32)
+    plane = pltpu.VMEM((1, 2, N, N, BY, BZ), f32)
+    made = 4 + 2 * 24 + 6 + 45
+    return pl.pallas_call(
+        reduce_kernel,
+        out_shape=[jax.ShapeDtypeStruct((BX, BY, BZ), f32)] * 2,
+        in_specs=[vm],
+        out_specs=[vm, vm],
+        scratch_shapes=[
+            pltpu.VMEM((N, 2, BX, 128, BZ), f32),
+            pltpu.VMEM((N, 2 * BX, N, N, BY, BZ), f32),
+            half, half, half, half, half, half, half, half, plane, plane, plane, plane,
+            pltpu.VMEM((N, 3, N, BY, BZ), f32), pltpu.VMEM((N, 3, N, BY, BZ), f32), pltpu.VMEM((2, N, N, BY, BZ), f32),
+            pltpu.VMEM((N, N, 3, BY, BZ), f32), pltpu.VMEM((N, N, 3, BY, BZ), f32), pltpu.VMEM((N, N, 2, BY, BZ), f32),
+            pltpu.SemaphoreType.DMA((made,)),
+            pltpu.SemaphoreType.DMA((made,)),
+            pltpu.SemaphoreType.REGULAR,
+        ],
+        compiler_params=pltpu.CompilerParams(collective_id=0, has_side_effects=True, vmem_limit_bytes=24 << 20),
+        name="reduce_grid",
+    )(grid)
+
+
 def shards(brick_ids, voxel_offset, fractions, normals, point_weight, tile_count):
     grid = splat(brick_ids[:, 0], tile_count, voxel_offset, fractions, normals, point_weight)
-    slabs, columns = lax.axis_size("gx"), lax.axis_size("yz")
-    grid = grid.reshape(2, PX, PY, BZ)[:, 1:1 + slabs * BX, BY:BY + columns * BY]
-    chunks = grid.reshape(2, slabs, BX, columns, BY, BZ).transpose(1, 3, 0, 2, 4, 5)
-    chunks = chunks.reshape(slabs * columns, 2, BX, BY, BZ)
-    mine = lax.psum_scatter(chunks, ("gx", "yz"), scatter_dimension=0, tiled=True)[0]
-    return mine[0], mine[1]
+    return tuple(reduce_grid(grid.reshape(2, PX, PY, BZ)))
 
 
 def solution(mesh):

time: 690 us -> 45.2 us (0.07)
  waiting for transfers between devices: 655 us -> 0 us
  Pallas kernels: 10.6 us -> 37.9 us
  between operations: 14.7 us -> 1.3 us
    reduce_scatter x1 -> x0, waiting for transfers between devices: 655 us -> none  [shards(): lax.psum_scatter(chunks, ('gx', 'yz'), scatter_dimension=0, tiled=True)[0]]
    pallas_call x0 -> x1, Pallas kernels: none -> 26.7 us  [reduce_grid(): pl.pallas_call(reduce_kernel, out_shape=[jax.ShapeDtypeStruct((BX, BY, BZ...]
  transfers between devices with their start and end apart: 1 -> 0, of which waited for: 1 -> 0; matrix products, arithmetic and copies ran while one was open for 0% -> 0% of each run, Pallas kernels for 0% -> 0%
where the time goes in v2:
time: 45.2 us; the launch traced here: 44.8 us
  Pallas kernels  37.9 us (84%)
  local copies, waits for them, and re-layouts  5.66 us (13%)
  between operations  1.3 us (3%)
    pallas_call x1, Pallas kernels, reduce_grid(): pl.pallas_call(reduce_kernel, out_shape=[jax.ShapeDtypeStruct((BX, BY, BZ...  26.7 us
    pallas_call x1, Pallas kernels, splat(): pl.pallas_call(splat_kernel, out_shape=jax.ShapeDtypeStruct((2 * PX * PY,...  11.2 us
    unnamed x12, local copies, waits for them, and re-layouts  5.66 us

profile of v2, /device:TPU:0, one launch (start us, length us, event | category | flops | bytes accessed | tf_op | source)
XLA Modules:
  0.0 44.8 jit_solution(13317727069844679636)
XLA Ops:
  1.3 0.0 copy-start
  1.3 1.0 %copy-done = f32[128,3,256]{2,0,1:T(8,128)S(1)} copy-done((f32[128,3,256]{2,0,1:T(8,128)S(1)}, f32[128,3,256]{2,0,1:T(8,128)}, u32[]{:S(2)}) %copy-start) | copy-done | bytes 393240
  2.3 0.0 copy-start.1
  2.3 1.0 %copy-done.1 = f32[128,3,256]{2,0,1:T(8,128)S(1)} copy-done((f32[128,3,256]{2,0,1:T(8,128)S(1)}, f32[128,3,256]{2,0,1:T(8,128)}, u32[]{:S(2)}) %copy-start.1) | copy-done | bytes 393240
  3.3 0.0 copy-start.2
  3.3 0.9 %copy-done.2 = s32[128,256]{1,0:T(8,128)S(1)} copy-done((s32[128,256]{1,0:T(8,128)S(1)}, s32[128,256]{1,0:T(8,128)}, u32[]{:S(2)}) %copy-start.2) | copy-done | bytes 131096
  4.2 0.0 copy-start.3
  4.2 0.9 %copy-done.3 = f32[128,256]{1,0:T(8,128)S(1)} copy-done((f32[128,256]{1,0:T(8,128)S(1)}, f32[128,256]{1,0:T(8,128)}, u32[]{:S(2)}) %copy-start.3) | copy-done | bytes 131096
  5.1 0.0 copy-start.4
  5.1 0.7 %copy-done.4 = s32[128,1]{0,1:T(1,128)S(1)} copy-done((s32[128,1]{0,1:T(1,128)S(1)}, s32[128,1]{0,1:T(1,128)}, u32[]{:S(2)}) %copy-start.4) | copy-done | bytes 536
  5.7 11.2 %splat.1 = f32[10944,128]{1,0:T(8,128)S(1)} custom-call(s32[128]{0:T(128)S(1)} %bitcast.7, s32[1]{0:T(128)S(6)} %copy.10.count_ref, s32[128,256]{1,0:T(8,128)S(1)} %copy-done.2, f32[3,128,256]{2,1,0:T(8,128)S(1)} %bitcast.5, f32[3,128,256]{2,1,0:T(8,128)S(1)} %bitcast.6, f32[128,256]{1,0:T(8,128)S(1)} %copy-done.3), custom_call_target="tpu_custom_call" | custom-call | tf_op jit(solution)/shard_map/splat/pallas_call | solution.py:168
  16.9 26.7 %reduce_grid.1 = (f32[4,8,128]{2,1,0:T(8,128)S(1)}, f32[4,8,128]{2,1,0:T(8,128)S(1)}) custom-call(f32[2,36,152,128]{3,2,1,0:T(8,128)S(1)} %bitcast.4), custom_call_target="tpu_custom_call" | custom-call | tf_op jit(solution)/shard_map/reduce_grid/pallas_call | solution.py:351
  43.6 0.6 %copy.11 = f32[4,8,128]{2,1,0:T(8,128)} copy(f32[4,8,128]{2,1,0:T(8,128)S(1)} %get-tuple-element.4) | data formatting | bytes 32768
  44.2 0.6 %copy.12 = f32[4,8,128]{2,1,0:T(8,128)} copy(f32[4,8,128]{2,1,0:T(8,128)S(1)} %get-tuple-element.5) | data formatting | bytes 32768
Async XLA Ops:
  1.3 1.0 %copy-start = (f32[128,3,256]{2,0,1:T(8,128)S(1)}, f32[128,3,256]{2,0,1:T(8,128)}, u32[]{:S(2)}) copy-start(f32[128,3,256]{2,0,1:T(8,128)} %param.8) | copy-start | bytes 1179652
  2.3 1.0 %copy-start.1 = (f32[128,3,256]{2,0,1:T(8,128)S(1)}, f32[128,3,256]{2,0,1:T(8,128)}, u32[]{:S(2)}) copy-start(f32[128,3,256]{2,0,1:T(8,128)} %param.9) | copy-start | bytes 1179652
  3.3 0.9 %copy-start.2 = (s32[128,256]{1,0:T(8,128)S(1)}, s32[128,256]{1,0:T(8,128)}, u32[]{:S(2)}) copy-start(s32[128,256]{1,0:T(8,128)} %off_ref.1) | copy-start | bytes 393220
  4.2 0.9 %copy-start.3 = (f32[128,256]{1,0:T(8,128)S(1)}, f32[128,256]{1,0:T(8,128)}, u32[]{:S(2)}) copy-start(f32[128,256]{1,0:T(8,128)} %s_ref.1) | copy-start | bytes 393220
  5.1 0.7 %copy-start.4 = (s32[128,1]{0,1:T(1,128)S(1)}, s32[128,1]{0,1:T(1,128)}, u32[]{:S(2)}) copy-start(s32[128,1]{0,1:T(1,128)} %param.6) | copy-start | bytes 1540

commit v3 on v2

v3 whole, which is shorter than its diff:
```python
import jax
import jax.numpy as jnp
from jax import lax
from jax.experimental import pallas as pl
from jax.experimental.pallas import tpu as pltpu
from jax.sharding import PartitionSpec as P

BX, BY, BZ = 4, 8, 128
PX, PY = 36, 152
U = 8
NONE = 128
SLOTS = 136

CZ0, CZ1, CZ2, WZ0, WZ1, WZ2, GZ0, GZ1, GZ2 = range(9)
CX, WX0, WX1, WX2, GX0, GX1, GX2 = range(9, 16)
CY, WY0, WY1, WY2, GY0, GY1, GY2 = range(16, 23)
QNX, QNY, QNZ, QS = range(23, 27)
NQ = 27


def spline(f):
    return ((0.5 * (1.0 - f) ** 2, 0.75 - (f - 0.5) ** 2, 0.5 * f * f),
            (f - 1.0, 1.0 - 2.0 * f, f))


def tile_build(t, q_ref):
    parts = [half_build(t, h, q_ref) for h in range(2)]
    return tuple(jnp.concatenate(p, 1) for p in zip(*parts))


def half_build(t, h, q_ref):
    def row(k):
        return q_ref[k, h, pl.ds(t, 8, stride=0), :]

    def pair(k):
        r = row(k)
        return jnp.concatenate([r, r], 0).astype(jnp.bfloat16)

    eight, sixteen = (8, 128), (16, 128)
    cz = [pair(CZ0 + k) for k in range(3)]
    wz = [pair(WZ0 + k) for k in range(3)]
    gz = [pair(GZ0 + k) for k in range(3)]
    zero = jnp.zeros(sixteen, jnp.bfloat16)
    zb, zd = [], []
    for i in range(BZ // 16):
        at = (lax.broadcasted_iota(jnp.int32, sixteen, 0) + 16 * i).astype(jnp.bfloat16)
        hit = [at == c for c in cz]
        zb.append(jnp.where(hit[0], wz[0], jnp.where(hit[1], wz[1], jnp.where(hit[2], wz[2], zero))))
        zd.append(jnp.where(hit[0], gz[0], jnp.where(hit[1], gz[1], jnp.where(hit[2], gz[2], zero))))
    zb = jnp.concatenate(zb, 0)
    zd = jnp.concatenate(zd, 0)

    at = lax.broadcasted_iota(jnp.int32, eight, 0)
    at = [(at - k).astype(jnp.float32) for k in range(3)]
    none = jnp.zeros(eight, jnp.float32)

    def spread(c, w0, g0):
        hit = [a == c for a in at]
        out = []
        for base in (w0, g0):
            v = [row(base + k) for k in range(3)]
            out.append(jnp.where(hit[0], v[0], jnp.where(hit[1], v[1], jnp.where(hit[2], v[2], none))))
        return out

    wx, gx = spread(row(CX), WX0, GX0)
    cy = row(CY)
    wy, gy = spread(cy, WY0, GY0)
    last, before = cy == float(BY - 1), cy == float(BY - 2)
    wy8 = jnp.where(last, row(WY1), jnp.where(before, row(WY2), none))
    gy8 = jnp.where(last, row(GY1), jnp.where(before, row(GY2), none))
    wy9 = jnp.where(last, row(WY2), none)
    gy9 = jnp.where(last, row(GY2), none)
    p = (row(QNX) * gx, row(QNY) * wx, row(QNZ) * wx, row(QS) * wx)
    a12, a3, a_s = [], [], []
    for x in range(BX + 2):
        b = [jnp.broadcast_to(v[x:x + 1], eight) for v in p]
        a12.append(b[0] * wy + b[1] * gy)
        a3.append(b[2] * wy)
        a_s.append(b[3] * wy)
    for w, g in ((wy8, gy8), (wy9, gy9)):
        a12.append(p[0] * w + p[1] * g)
        a3.append(p[2] * w)
        a_s.append(p[3] * w)
    lhs1 = jnp.concatenate(a12 + a_s, 0).astype(jnp.bfloat16)
    lhs2 = jnp.concatenate(a3, 0).astype(jnp.bfloat16)
    return lhs1, lhs2, zb, zd


def contract(lhs1, lhs2, zb, zd):
    nt = (((1,), (1,)), ((), ()))
    r1 = lax.dot_general(lhs1, zb, nt, preferred_element_type=jnp.float32)
    r2 = lax.dot_general(lhs2, zd, nt, preferred_element_type=jnp.float32)
    return r1[:64] + r2, r1[64:]


def add_in(slab, column, res, out_ref):
    x0 = slab * BX
    y0 = column * BY + 7
    for f in range(2):
        base = (f * PX + x0) * PY + y0
        for x in range(BX + 2):
            r = pl.ds(base + x * PY, 8)
            out_ref[r, :] += res[f][8 * x:8 * x + 8]
        for k in range(2):
            r = pl.ds(base + 8 + k, 8, stride=PY)
            out_ref[r, :] += res[f][48 + 8 * k:56 + 8 * k]


def prepare_kernel(dest_hbm, count_hbm, off_hbm, frac_hbm, norm_hbm, s_hbm, grid_ref, q_ref, first_ref,
                   dest_ref, count_ref, off_ref, frac_ref, norm_ref, s_ref, list_ref, sems):
    pairs = ((count_hbm, count_ref), (dest_hbm, dest_ref), (off_hbm, off_ref), (frac_hbm, frac_ref), (norm_hbm, norm_ref),
             (s_hbm, s_ref))
    loads = [pltpu.make_async_copy(src, dst, sems.at[i]) for i, (src, dst) in enumerate(pairs)]
    for load in loads:
        load.start()
    grid_ref[...] = jnp.zeros_like(grid_ref)
    q_ref[:, :, pl.ds(NONE, 8), :] = jnp.zeros((NQ, 2, 8, 128), jnp.float32)

    def clear(i, _):
        for k in range(8):
            first_ref[i * 8 + k] = NONE
        return 0

    lax.fori_loop(0, NONE // 8, clear, 0)
    for load in loads:
        load.wait()
    count = count_ref[0]

    def group(g, seconds):
        r = pl.ds(pl.multiple_of(g * 8, 8), 8)

        def put(k, value):
            for h in range(2):
                q_ref[k, h, r, :] = value[:, h * 128:h * 128 + 128]

        off = off_ref[r, :]
        valid = g * 8 + lax.broadcasted_iota(jnp.int32, off.shape, 0) < count
        cz = (off & (BZ - 1)).astype(jnp.float32)
        put(CZ0, cz - 1.0)
        put(CZ1, cz)
        put(CZ2, cz + 1.0)
        put(CX, (off >> 10).astype(jnp.float32))
        put(CY, ((off >> 7) & (BY - 1)).astype(jnp.float32))
        for dim, w0, g0 in ((0, WX0, GX0), (1, WY0, GY0), (2, WZ0, GZ0)):
            w, s = spline(frac_ref[dim, r, :])
            for k in range(3):
                put(w0 + k, w[k])
                put(g0 + k, s[k])
        for k in range(3):
            put(QNX + k, jnp.where(valid, norm_ref[k, r, :], 0.0))
        put(QS, jnp.where(valid, s_ref[r, :], 0.0))
        for k in range(8):
            t = g * 8 + k
            brick = dest_ref[t]
            known = first_ref[brick]
            real = t < count
            again = jnp.logical_and(real, known < NONE)
            first_ref[brick] = jnp.where(jnp.logical_and(real, known == NONE), t, known)
            list_ref[seconds] = t
            seconds = seconds + again.astype(jnp.int32)
        return seconds

    seconds = lax.fori_loop(0, NONE // 8, group, 0)
    for k in range(U):
        list_ref[seconds + k] = NONE

    def more(i, _):
        ts = [list_ref[i * U + u] for u in range(U)]
        sums = [contract(*tile_build(t, q_ref)) for t in ts]
        for t, each in zip(ts, sums):
            brick = dest_ref[jnp.minimum(t, NONE - 1)]
            add_in(brick // 16, brick % 16, each, grid_ref)
        return 0

    lax.fori_loop(0, (seconds + U - 1) // U, more, 0)


def prepare(dest, count, off, frac, norm, s):
    tiles, n = off.shape
    hbm = pl.BlockSpec(memory_space=pltpu.HBM)
    f32 = jnp.float32
    return pl.pallas_call(
        prepare_kernel,
        out_shape=[jax.ShapeDtypeStruct((2 * PX * PY, BZ), f32), jax.ShapeDtypeStruct((NQ, 2, SLOTS, 128), f32),
                   jax.ShapeDtypeStruct((tiles,), jnp.int32)],
        in_specs=[hbm] * 6,
        out_specs=[pl.BlockSpec(memory_space=pltpu.VMEM)] * 2 + [pl.BlockSpec(memory_space=pltpu.SMEM)],
        scratch_shapes=[
            pltpu.SMEM((tiles,), jnp.int32), pltpu.SMEM((1,), jnp.int32), pltpu.VMEM((tiles, n), jnp.int32),
            pltpu.VMEM((3, tiles, n), f32), pltpu.VMEM((3, tiles, n), f32), pltpu.VMEM((tiles, n), f32),
            pltpu.SMEM((tiles + 2 * U,), jnp.int32), pltpu.SemaphoreType.DMA((6,)),
        ],
        compiler_params=pltpu.CompilerParams(vmem_limit_bytes=16 << 20),
        name="prepare",
    )(dest, count, off, jnp.transpose(frac, (1, 0, 2)), jnp.transpose(norm, (1, 0, 2)), s)


N = 4
MESH = pl.DeviceIdType.MESH


class Copies:
    def __init__(self, send_sems, recv_sems):
        self.send_sems, self.recv_sems = send_sems, recv_sems
        self.made = []

    def start(self, src, dst, device):
        i = len(self.made)
        copy = pltpu.make_async_remote_copy(
            src_ref=src, dst_ref=dst, send_sem=self.send_sems.at[i], recv_sem=self.recv_sems.at[i],
            device_id=device, device_id_type=MESH)
        copy.start()
        self.made.append(copy)
        return copy

    def finish(self):
        for copy in self.made:
            copy.wait_send()


def splat_kernel(first_ref, q_ref, start_ref, rhs_ref, screen_ref, grid_ref, pair_ref, sum_ref,
                 xa, xb, xc, xr, ya, yb, yc, yr, za, zb, zc, zr, sx, sy, sz, rx, ry, rz, send_sems, recv_sems, ready_sem):
    slab, column = lax.axis_index("gx"), lax.axis_index("yz")
    pz, core = slab // 2, slab % 2
    py, px = column // N, column % N

    def device(dz=0, dy=0, dx=0):
        return (((pz + dz) % N) * 2 + core, ((py + dy) % N) * N + (px + dx) % N)

    other = (pz * 2 + 1 - core, column)
    lines = [device(**{axis: k}) for axis in ("dz", "dy", "dx") for k in range(1, N)]
    barrier = pltpu.get_barrier_semaphore()
    for peer in [other] + lines:
        pl.semaphore_signal(barrier, inc=1, device_id=peer, device_id_type=MESH)

    flat = 2 * PX * PY

    def fetch(i, _):
        r = pl.ds(pl.multiple_of(i * 96, 96), 96)
        grid_ref[r, :] = start_ref[r, :]
        return 0

    lax.fori_loop(0, flat // 96, fetch, 0)

    def bricks(i, _):
        bx = (2 * pz + 3 + i // 2) % (2 * N)
        ys = [(i % 2) * U + u for u in range(U)]
        sums = [contract(*tile_build(first_ref[bx * 16 + y], q_ref)) for y in ys]
        for y, each in zip(ys, sums):
            add_in(bx, y, each, grid_ref)
        return 0

    copies = Copies(send_sems, recv_sems)
    grid = grid_ref.reshape(2, PX, PY, BZ)
    order = (2, 3, 0, 1)
    pair = {}

    def send_pair(j):
        rows = pl.ds(1 + BX * (((pz + j) % N) * 2 + 1 - core), BX)
        pair[j] = copies.start(grid.at[:, rows, pl.ds(BY, 128), :], pair_ref.at[j], other)

    def data_x(j, h, d):
        return (j, slice(0, 3), slice(2 * h, 2 * h + 2), (px + d) % N)

    def data_y(j, h, d):
        return (j, slice(3, 6), (py + d) % N, slice(2 * h, 2 * h + 2))

    def data_z(j, h, d):
        return (d % N, 6 + h)

    parts = {"x": (data_x, "dx", xa, xb, xc, xr), "y": (data_y, "dy", ya, yb, yc, yr), "z": (data_z, "dz", za, zb, zc, zr)}
    first, second, third = {}, {}, {}

    def toward(name, way):
        return device(**{parts[name][1]: 1 if way == 0 else N - 1})

    def send_far(name, j):
        data, _, a, _, _, _ = parts[name]
        for way in range(2):
            first[name, j, way] = copies.start(sum_ref.at[data(j, way, 2)], a.at[j, way], toward(name, way))

    def send_near(name, j, ways=(0, 1)):
        data, _, _, b, _, _ = parts[name]
        for way in ways:
            second[name, j, way] = copies.start(sum_ref.at[data(j, 1 - way, 1 if way == 0 else N - 1)], b.at[j, way],
                                                toward(name, way))

    def relay(name, j, ways=(0, 1)):
        data, _, a, _, c, r = parts[name]
        for way in ways:
            first[name, j, way].wait_recv()
            r[j, way] = a[j, way] + sum_ref[data(j, way, 1 if way == 0 else N - 1)]
            third[name, j, way] = copies.start(r.at[j, way], c.at[j, way], toward(name, way))

    def combine(j):
        pair[j].wait_recv()
        rows = 1 + BX * (((pz + j) % N) * 2 + core)
        for f in range(2):
            def add_plane(x, _, f=f):
                total = grid[f, rows + x, pl.ds(BY, 128), :] + pair_ref[j, f, x]
                sum_ref[j, BX * f + x] = total.reshape(N, N, BY, BZ)
                return 0
            lax.fori_loop(0, BX, add_plane, 0)
        send_far("x", j)
        send_far("y", j)
        if j == 2:
            send_far("z", 0)
        if j == 1:
            relay("z", 0, (0,))
            send_near("z", 0, (0,))
        if j == 3:
            send_near("z", 0, (1,))
        send_near("x", j)
        send_near("y", j)

    def joined(name, j, own):
        _, _, _, b, c, _ = parts[name]
        for way in range(2):
            second[name, j, way].wait_recv()
            third[name, j, way].wait_recv()
        return [own(h) + c[j, h] + b[j, 1 - h] for h in range(2)]

    last = []

    def owners(j):
        for name, data, s, r in (("x", data_x, sx, rx), ("y", data_y, sy, ry)):
            low, high = joined(name, j, lambda h: sum_ref[data(j, h, 0)])
            s[j, :, 0:2] = low
            s[j, :, 2:4] = high
            for m in (2, 1, 3, 0):
                if (j, m) == (0, 0):
                    continue
                if name == "x":
                    where, peer = s.at[j, :, (py + m) % N], device(dz=j, dy=m)
                else:
                    where, peer = s.at[j, :, (px + m) % N], device(dz=j, dx=m)
                last.append(copies.start(where, r.at[j, m], peer))

    lax.fori_loop(0, 8, bricks, 0)
    pl.semaphore_wait(barrier, 1 + len(lines))
    for peer in lines:
        pl.semaphore_signal(ready_sem, inc=1, device_id=peer, device_id_type=MESH)
    send_pair(2)
    lax.fori_loop(8, 12, bricks, 0)
    send_pair(3)
    combine(2)
    lax.fori_loop(12, 16, bricks, 0)
    send_pair(0)
    send_pair(1)
    combine(3)
    relay("x", 2)
    relay("y", 2)
    relay("z", 0, (1,))
    combine(0)
    relay("x", 3)
    relay("y", 3)
    combine(1)
    pl.semaphore_wait(ready_sem, len(lines))
    owners(2)
    relay("x", 0)
    relay("y", 0)
    owners(3)
    relay("x", 1)
    relay("y", 1)
    owners(0)
    low, high = joined("z", 0, lambda h: sum_ref[data_z(0, h, 0)])
    sz[0] = low
    sz[1] = high
    for j in order:
        for m in (2, 1, 3, 0):
            if (j, m) != (0, 0):
                last.append(copies.start(sz.at[:, (py + j) % N, (px + m) % N], rz.at[j, m], device(dy=j, dx=m)))
    owners(1)
    for copy in last:
        copy.wait_recv()

    def total(own, r):
        for j in range(N):
            for m in range(N):
                if (j, m) != (0, 0):
                    own = own + r[j, m]
        return own

    fx = total(sx[0, :, py], rx)
    fy = total(sy[0, :, px], ry)
    fz = total(sz[:, py, px], rz)
    rhs_ref[0:3] = fx
    rhs_ref[3] = fy[0]
    screen_ref[0:2] = fy[1:3]
    screen_ref[2:4] = fz
    copies.finish()


def splat(first, q, start):
    vm = pl.BlockSpec(memory_space=pltpu.VMEM)
    f32 = jnp.float32
    half = pltpu.VMEM((N, 2, 3, 2, BY, BZ), f32)
    plane = pltpu.VMEM((1, 2, N, N, BY, BZ), f32)
    made = 4 + 2 * 24 + 6 + 45
    return pl.pallas_call(
        splat_kernel,
        out_shape=[jax.ShapeDtypeStruct((BX, BY, BZ), f32)] * 2,
        in_specs=[pl.BlockSpec(memory_space=pltpu.SMEM), vm, vm],
        out_specs=[vm, vm],
        scratch_shapes=[
            pltpu.VMEM((2 * PX * PY, BZ), f32),
            pltpu.VMEM((N, 2, BX, 128, BZ), f32),
            pltpu.VMEM((N, 2 * BX, N, N, BY, BZ), f32),
            half, half, half, half, half, half, half, half, plane, plane, plane, plane,
            pltpu.VMEM((N, 3, N, BY, BZ), f32), pltpu.VMEM((N, 3, N, BY, BZ), f32), pltpu.VMEM((2, N, N, BY, BZ), f32),
            pltpu.VMEM((N, N, 3, BY, BZ), f32), pltpu.VMEM((N, N, 3, BY, BZ), f32), pltpu.VMEM((N, N, 2, BY, BZ), f32),
            pltpu.SemaphoreType.DMA((made,)),
            pltpu.SemaphoreType.DMA((made,)),
            pltpu.SemaphoreType.REGULAR,
        ],
        compiler_params=pltpu.CompilerParams(collective_id=0, has_side_effects=True, vmem_limit_bytes=28 << 20),
        name="splat",
    )(first, q, start)


def shards(brick_ids, voxel_offset, fractions, normals, point_weight, tile_count):
    grid, q, first = prepare(brick_ids[:, 0], tile_count, voxel_offset, fractions, normals, point_weight)
    return tuple(splat(first, q, grid))


def solution(mesh):
    return jax.shard_map(
        shards,
        mesh=mesh,
        in_specs=(
            P(("gx", "yz"), None),
            P(("gx", "yz"), None),
            P(("gx", "yz"), None, None),
            P(("gx", "yz"), None, None),
            P(("gx", "yz"), None),
            P(("gx", "yz")),
        ),
        out_specs=(P("gx", "yz", None), P("gx", "yz", None)),
        check_vma=False,
    )
```

time: 45.2 us -> 44.8 us (level)
  no operation moved by 1% of the time
where the time goes in v3:
time: 44.8 us; the launch traced here: 44.5 us
  Pallas kernels  37.6 us (84%)
  local copies, waits for them, and re-layouts  5.66 us (13%)
  between operations  1.31 us (3%)
    pallas_call x1, Pallas kernels, splat(): pl.pallas_call(splat_kernel, out_shape=[jax.ShapeDtypeStruct((BX, BY, BZ)...  34.1 us
    unnamed x12, local copies, waits for them, and re-layouts  5.66 us
    pallas_call x1, Pallas kernels, prepare(): pl.pallas_call(prepare_kernel, out_shape=[jax.ShapeDtypeStruct((2 * PX *...  3.42 us

profile of v3, /device:TPU:0, one launch (start us, length us, event | category | flops | bytes accessed | tf_op | source)
XLA Modules:
  0.0 44.5 jit_solution(3116941157720830893)
XLA Ops:
  1.3 0.0 copy-start
  1.3 1.0 %copy-done = f32[128,3,256]{2,0,1:T(8,128)S(1)} copy-done((f32[128,3,256]{2,0,1:T(8,128)S(1)}, f32[128,3,256]{2,0,1:T(8,128)}, u32[]{:S(2)}) %copy-start) | copy-done | bytes 393240
  2.3 0.0 copy-start.1
  2.3 1.0 %copy-done.1 = f32[128,3,256]{2,0,1:T(8,128)S(1)} copy-done((f32[128,3,256]{2,0,1:T(8,128)S(1)}, f32[128,3,256]{2,0,1:T(8,128)}, u32[]{:S(2)}) %copy-start.1) | copy-done | bytes 393240
  3.3 0.0 copy-start.2
  3.3 0.9 %copy-done.2 = s32[128,256]{1,0:T(8,128)S(1)} copy-done((s32[128,256]{1,0:T(8,128)S(1)}, s32[128,256]{1,0:T(8,128)}, u32[]{:S(2)}) %copy-start.2) | copy-done | bytes 131096
  4.2 0.0 copy-start.3
  4.2 0.9 %copy-done.3 = f32[128,256]{1,0:T(8,128)S(1)} copy-done((f32[128,256]{1,0:T(8,128)S(1)}, f32[128,256]{1,0:T(8,128)}, u32[]{:S(2)}) %copy-start.3) | copy-done | bytes 131096
  5.1 0.0 copy-start.4
  5.1 0.7 %copy-done.4 = s32[128,1]{0,1:T(1,128)S(1)} copy-done((s32[128,1]{0,1:T(1,128)S(1)}, s32[128,1]{0,1:T(1,128)}, u32[]{:S(2)}) %copy-start.4) | copy-done | bytes 536
  5.7 3.4 %prepare.1 = (f32[10944,128]{1,0:T(8,128)S(1)}, f32[27,2,136,128]{3,2,1,0:T(8,128)S(1)}, s32[128]{0:T(128)S(1)}) custom-call(s32[128]{0:T(128)S(1)} %bitcast.5, s32[1]{0:T(128)S(6)} %copy.10.count_hbm, s32[128,256]{1,0:T(8,128)S(1)} %copy-done.2, f32[3,128,256]{2,1,0:T(8,128)S(1)} %bitcast.3, f32[3,128,256]{2,1,0:T(8,128)S(1)} %bitcast.4, ...), custom_call_target="tpu_custom_call" | custom-call | tf_op jit(solution)/shard_map/prepare/pallas_call | solution.py:182
  9.2 34.1 %splat.1 = (f32[4,8,128]{2,1,0:T(8,128)S(1)}, f32[4,8,128]{2,1,0:T(8,128)S(1)}) custom-call(s32[128]{0:T(128)S(1)} %get-tuple-element.5.first_ref, f32[27,2,136,128]{3,2,1,0:T(8,128)S(1)} %get-tuple-element.6.q_ref, f32[10944,128]{1,0:T(8,128)S(1)} %get-tuple-element.7.start_ref), custom_call_target="tpu_custom_call" | custom-call | tf_op jit(solution)/shard_map/splat/pallas_call | solution.py:400
  43.3 0.6 %copy.11 = f32[4,8,128]{2,1,0:T(8,128)} copy(f32[4,8,128]{2,1,0:T(8,128)S(1)} %get-tuple-element.10) | data formatting | bytes 32768
  43.9 0.6 %copy.12 = f32[4,8,128]{2,1,0:T(8,128)} copy(f32[4,8,128]{2,1,0:T(8,128)S(1)} %get-tuple-element.11) | data formatting | bytes 32768
Async XLA Ops:
  1.3 1.0 %copy-start = (f32[128,3,256]{2,0,1:T(8,128)S(1)}, f32[128,3,256]{2,0,1:T(8,128)}, u32[]{:S(2)}) copy-start(f32[128,3,256]{2,0,1:T(8,128)} %param.8) | copy-start | bytes 1179652
  2.3 1.0 %copy-start.1 = (f32[128,3,256]{2,0,1:T(8,128)S(1)}, f32[128,3,256]{2,0,1:T(8,128)}, u32[]{:S(2)}) copy-start(f32[128,3,256]{2,0,1:T(8,128)} %param.9) | copy-start | bytes 1179652
  3.3 0.9 %copy-start.2 = (s32[128,256]{1,0:T(8,128)S(1)}, s32[128,256]{1,0:T(8,128)}, u32[]{:S(2)}) copy-start(s32[128,256]{1,0:T(8,128)} %off_hbm.1) | copy-start | bytes 393220
  4.2 0.9 %copy-start.3 = (f32[128,256]{1,0:T(8,128)S(1)}, f32[128,256]{1,0:T(8,128)}, u32[]{:S(2)}) copy-start(f32[128,256]{1,0:T(8,128)} %s_hbm.1) | copy-start | bytes 393220
  5.1 0.7 %copy-start.4 = (s32[128,1]{0,1:T(1,128)S(1)}, s32[128,1]{0,1:T(1,128)}, u32[]{:S(2)}) copy-start(s32[128,1]{0,1:T(1,128)} %param.6) | copy-start | bytes 1540

commit v4 on v3

v4 whole, which is shorter than its diff:
```python
import jax
import jax.numpy as jnp
from jax import lax
from jax.experimental import pallas as pl
from jax.experimental.pallas import tpu as pltpu
from jax.sharding import PartitionSpec as P

BX, BY, BZ = 4, 8, 128
PX, PY = 36, 152
V = 8

CZ, WZ, GZ = 0, 3, 6
WY, GY = 9, 19
PXX, PXY, PXZ, PXS = 29, 37, 45, 53
HALF = 61
ROWS = 123
NONE = 128


def spline(f):
    return ((0.5 * (1.0 - f) ** 2, 0.75 - (f - 0.5) ** 2, 0.5 * f * f),
            (f - 1.0, 1.0 - 2.0 * f, f))


def slots(cell, cells, values):
    hit = [cell == c for c in range(cells)]
    out = []
    for i in range(cells + 2):
        total = 0.0
        for k in range(3):
            if 0 <= i - k < cells:
                total = jnp.where(hit[i - k], values[k], total)
        out.append(total)
    return out


def tile_build(t, q_ref):
    parts = [half_build(t * ROWS + h * HALF, q_ref) for h in range(2)]
    return tuple(jnp.concatenate(p, 1) for p in zip(*parts))


def half_build(base, q_ref):
    def row(k):
        return q_ref[pl.ds(base + k, 8, stride=0), :]

    def rows(k):
        return q_ref[pl.ds(base + k, 8), :]

    def pair(k):
        r = row(k)
        return jnp.concatenate([r, r], 0).astype(jnp.bfloat16)

    sixteen = (16, 128)
    cz = [pair(CZ + k) for k in range(3)]
    wz = [pair(WZ + k) for k in range(3)]
    gz = [pair(GZ + k) for k in range(3)]
    zero = jnp.zeros(sixteen, jnp.bfloat16)
    zb, zd = [], []
    for i in range(BZ // 16):
        at = (lax.broadcasted_iota(jnp.int32, sixteen, 0) + 16 * i).astype(jnp.bfloat16)
        hit = [at == c for c in cz]
        zb.append(jnp.where(hit[0], wz[0], jnp.where(hit[1], wz[1], jnp.where(hit[2], wz[2], zero))))
        zd.append(jnp.where(hit[0], gz[0], jnp.where(hit[1], gz[1], jnp.where(hit[2], gz[2], zero))))
    zb = jnp.concatenate(zb, 0)
    zd = jnp.concatenate(zd, 0)

    wy, gy = rows(WY), rows(GY)
    a12, a3, a_s = [], [], []
    for x in range(BX + 2):
        a12.append(row(PXX + x) * wy + row(PXY + x) * gy)
        a3.append(row(PXZ + x) * wy)
        a_s.append(row(PXS + x) * wy)
    p = [rows(k) for k in (PXX, PXY, PXZ, PXS)]
    for y in (BY, BY + 1):
        w, g = row(WY + y), row(GY + y)
        a12.append(p[0] * w + p[1] * g)
        a3.append(p[2] * w)
        a_s.append(p[3] * w)
    lhs1 = jnp.concatenate(a12 + a_s, 0).astype(jnp.bfloat16)
    lhs2 = jnp.concatenate(a3, 0).astype(jnp.bfloat16)
    return lhs1, lhs2, zb, zd


def contract(lhs1, lhs2, zb, zd):
    nt = (((1,), (1,)), ((), ()))
    r1 = lax.dot_general(lhs1, zb, nt, preferred_element_type=jnp.float32)
    r2 = lax.dot_general(lhs2, zd, nt, preferred_element_type=jnp.float32)
    return r1[:64] + r2, r1[64:]


def add_in(slab, column, res, out_ref):
    x0 = slab * BX
    y0 = column * BY + 7
    for f in range(2):
        base = (f * PX + x0) * PY + y0
        for x in range(BX + 2):
            r = pl.ds(base + x * PY, 8)
            out_ref[r, :] += res[f][8 * x:8 * x + 8]
        for k in range(2):
            r = pl.ds(base + 8 + k, 8, stride=PY)
            out_ref[r, :] += res[f][48 + 8 * k:56 + 8 * k]


def prepare_kernel(count_ref, dest_hbm, off_hbm, frac_hbm, norm_hbm, s_hbm, grid_ref, q_ref, first_ref,
                   dest_ref, off_ref, frac_ref, norm_ref, s_ref, list_ref, sems):
    pairs = ((dest_hbm, dest_ref), (off_hbm, off_ref), (frac_hbm, frac_ref), (norm_hbm, norm_ref),
             (s_hbm, s_ref))
    loads = [pltpu.make_async_copy(src, dst, sems.at[i]) for i, (src, dst) in enumerate(pairs)]
    for load in loads:
        load.start()
    grid_ref[...] = jnp.zeros_like(grid_ref)
    q_ref[pl.ds(NONE * ROWS, 128), :] = jnp.zeros((128, 128), jnp.float32)

    def clear(i, _):
        for k in range(8):
            first_ref[i * 8 + k] = NONE
        return 0

    lax.fori_loop(0, NONE // 8, clear, 0)
    for load in loads:
        load.wait()
    count = count_ref[0]

    def group(g, seconds):
        r = pl.ds(pl.multiple_of(g * 8, 8), 8)
        valid = g * 8 + lax.broadcasted_iota(jnp.int32, (8, 128), 0) < count
        for h in range(2):
            lanes = slice(h * 128, h * 128 + 128)

            def put(k, value):
                q_ref[pl.ds(g * 8 * ROWS + h * HALF + k, 8, stride=ROWS), :] = value

            off = off_ref[r, lanes]
            nx, ny, nz = (jnp.where(valid, norm_ref[k, r, lanes], 0.0) for k in range(3))
            s = jnp.where(valid, s_ref[r, lanes], 0.0)
            cell = off & (BZ - 1)
            w, slope = spline(frac_ref[2, r, lanes])
            for k in range(3):
                put(CZ + k, (cell + (k - 1)).astype(jnp.float32))
                put(WZ + k, w[k])
                put(GZ + k, slope[k])
            w, slope = spline(frac_ref[1, r, lanes])
            cell = (off >> 7) & (BY - 1)
            for base, values in ((WY, w), (GY, slope)):
                for i, value in enumerate(slots(cell, BY, values)):
                    put(base + i, value)
            w, slope = spline(frac_ref[0, r, lanes])
            cell = off >> 10
            wx, gx = slots(cell, BX, w), slots(cell, BX, slope)
            for i in range(BX + 2):
                put(PXX + i, nx * gx[i])
                put(PXY + i, ny * wx[i])
                put(PXZ + i, nz * wx[i])
                put(PXS + i, s * wx[i])
            none = jnp.zeros((8, 128), jnp.float32)
            for base in (PXX, PXY, PXZ, PXS):
                put(base + BX + 2, none)
                put(base + BX + 3, none)
        for k in range(8):
            t = g * 8 + k
            brick = dest_ref[t]
            known = first_ref[brick]
            real = t < count
            again = jnp.logical_and(real, known < NONE)
            first_ref[brick] = jnp.where(jnp.logical_and(real, known == NONE), t, known)
            list_ref[seconds] = t
            seconds = seconds + again.astype(jnp.int32)
        return seconds

    seconds = lax.fori_loop(0, NONE // 8, group, 0)
    for k in range(V):
        list_ref[seconds + k] = NONE

    def more(i, _):
        ts = [list_ref[i * V + u] for u in range(V)]
        sums = [contract(*tile_build(t, q_ref)) for t in ts]
        for t, each in zip(ts, sums):
            brick = dest_ref[jnp.minimum(t, NONE - 1)]
            add_in(brick // 16, brick % 16, each, grid_ref)
        return 0

    lax.fori_loop(0, (seconds + V - 1) // V, more, 0)


def prepare(dest, count, off, frac, norm, s):
    tiles, n = off.shape
    hbm = pl.BlockSpec(memory_space=pltpu.HBM)
    f32 = jnp.float32
    return pl.pallas_call(
        prepare_kernel,
        out_shape=[jax.ShapeDtypeStruct((2 * PX * PY, BZ), f32), jax.ShapeDtypeStruct((NONE * ROWS + 128, 128), f32),
                   jax.ShapeDtypeStruct((tiles,), jnp.int32)],
        in_specs=[pl.BlockSpec(memory_space=pltpu.SMEM)] + [hbm] * 5,
        out_specs=[pl.BlockSpec(memory_space=pltpu.VMEM)] * 2 + [pl.BlockSpec(memory_space=pltpu.SMEM)],
        scratch_shapes=[
            pltpu.SMEM((tiles,), jnp.int32), pltpu.VMEM((tiles, n), jnp.int32),
            pltpu.VMEM((3, tiles, n), f32), pltpu.VMEM((3, tiles, n), f32), pltpu.VMEM((tiles, n), f32),
            pltpu.SMEM((tiles + 2 * V,), jnp.int32), pltpu.SemaphoreType.DMA((5,)),
        ],
        compiler_params=pltpu.CompilerParams(vmem_limit_bytes=22 << 20),
        name="prepare",
    )(count, *(pltpu.with_memory_space_constraint(x, pltpu.HBM) for x in
               (dest, off, jnp.transpose(frac, (1, 0, 2)), jnp.transpose(norm, (1, 0, 2)), s)))


N = 4
MESH = pl.DeviceIdType.MESH


class Copies:
    def __init__(self, send_sems, recv_sems):
        self.send_sems, self.recv_sems = send_sems, recv_sems
        self.made = []

    def start(self, src, dst, device):
        i = len(self.made)
        copy = pltpu.make_async_remote_copy(
            src_ref=src, dst_ref=dst, send_sem=self.send_sems.at[i], recv_sem=self.recv_sems.at[i],
            device_id=device, device_id_type=MESH)
        copy.start()
        self.made.append(copy)
        return copy

    def finish(self):
        for copy in self.made:
            copy.wait_send()


PARTS = (3, 3, 2)


def splat_kernel(first_ref, q_ref, start_ref, rhs_ref, screen_ref, grid_ref, pair_ref, sum_ref,
                 xa, xb, xc, xr, ya, yb, yc, yr, za, zb, zc, zr, sx, sy, sz, rx, ry, rz, send_sems, recv_sems, ready_sem):
    slab, column = lax.axis_index("gx"), lax.axis_index("yz")
    pz, core = slab // 2, slab % 2
    py, px = column // N, column % N

    def device(dz=0, dy=0, dx=0):
        return (((pz + dz) % N) * 2 + core, ((py + dy) % N) * N + (px + dx) % N)

    other = (pz * 2 + 1 - core, column)
    lines = [device(**{axis: k}) for axis in ("dz", "dy", "dx") for k in range(1, N)]
    barrier = pltpu.get_barrier_semaphore()
    for peer in [other] + lines:
        pl.semaphore_signal(barrier, inc=1, device_id=peer, device_id_type=MESH)

    def fetch(i, _):
        r = pl.ds(pl.multiple_of(i * 96, 96), 96)
        grid_ref[r, :] = start_ref[r, :]
        return 0

    lax.fori_loop(0, 2 * PX * PY // 96, fetch, 0)

    def bricks(place):
        def step(i, _):
            ys = [(N * py + 2 * N + N * N + place(2 * i + k)) % (N * N) for k in range(2)]
            places = [(x, y) for y in ys for x in range(2 * N)]
            sums = [contract(*tile_build(first_ref[x * 16 + y], q_ref)) for x, y in places]
            for (x, y), each in zip(places, sums):
                add_in(x, y, each, grid_ref)
            return 0
        return step

    copies = Copies(send_sems, recv_sems)
    grid = grid_ref.reshape(2, PX, PY, BZ)
    pair = {}

    def rows_of(o):
        return pl.ds(pl.multiple_of(BY + N * BY * ((py + o) % N), BY), N * BY)

    def cells_of(j, which):
        return 1 + BX * (((pz + j) % N) * 2 + which)

    def send_pair(o):
        for j in range(N):
            pair[o, j] = copies.start(grid.at[:, pl.ds(cells_of(j, 1 - core), BX), rows_of(o), :], pair_ref.at[o, j], other)

    nx, ny, nz = PARTS
    xs, ys, zs = slice(0, nx), slice(nx, nx + ny), slice(nx + ny, nx + ny + nz)

    def data_x(o, h, d):
        return (o, slice(2 * h, 2 * h + 2), xs, (px + d) % N)

    def data_y(o, h, d):
        return (d % N, slice(2 * h, 2 * h + 2), ys)

    def data_z(o, h, d):
        return (o, d % N, zs, slice(2 * h, 2 * h + 2))

    parts = {"x": (data_x, "dx", xa, xb, xc, xr), "y": (data_y, "dy", ya, yb, yc, yr), "z": (data_z, "dz", za, zb, zc, zr)}
    first, second, third = {}, {}, {}

    def toward(name, way):
        return device(**{parts[name][1]: 1 if way == 0 else N - 1})

    def send_far(name, o):
        data, _, a, _, _, _ = parts[name]
        for way in range(2):
            first[name, o, way] = copies.start(sum_ref.at[data(o, way, 2)], a.at[o, way], toward(name, way))

    def send_near(name, o, ways=(0, 1)):
        data, _, _, b, _, _ = parts[name]
        for way in ways:
            second[name, o, way] = copies.start(sum_ref.at[data(o, 1 - way, 1 if way == 0 else N - 1)], b.at[o, way],
                                                toward(name, way))

    def relay(name, o, ways=(0, 1)):
        data, _, a, _, c, r = parts[name]
        for way in ways:
            first[name, o, way].wait_recv()
            r[o, way] = a[o, way] + sum_ref[data(o, way, 1 if way == 0 else N - 1)]
            third[name, o, way] = copies.start(r.at[o, way], c.at[o, way], toward(name, way))

    def combine(o):
        for j in range(N):
            pair[o, j].wait_recv()
            for f in range(2):
                for x in range(BX):
                    total = grid[f, cells_of(j, core) + x, rows_of(o), :] + pair_ref[o, j, f, x]
                    sum_ref[o, j, BX * f + x] = total.reshape(N, BY, BZ)
        send_far("x", o)
        send_far("z", o)
        if o == 2:
            send_far("y", 0)
        send_near("x", o)
        send_near("z", o)
        if o == 3:
            relay("y", 0, (1,))
            send_near("y", 0, (1,))
        if o == 1:
            relay("y", 0, (0,))
            send_near("y", 0, (0,))

    def joined(name, o, own):
        _, _, _, b, c, _ = parts[name]
        for way in range(2):
            second[name, o, way].wait_recv()
            third[name, o, way].wait_recv()
        return [own(h) + c[o, h] + b[o, 1 - h] for h in range(2)]

    last = []

    def owners(o):
        sx[o, 0:2], sx[o, 2:4] = joined("x", o, lambda h: sum_ref[data_x(o, h, 0)])
        sz[o, :, 0:2], sz[o, :, 2:4] = joined("z", o, lambda h: sum_ref[data_z(o, h, 0)])
        for k in (2, 1, 3, 0):
            if (o, k) != (0, 0):
                last.append(copies.start(sx.at[o, k], rx.at[o, k], device(dy=o, dz=k)))
                last.append(copies.start(sz.at[o, :, (px + k) % N], rz.at[o, k], device(dy=o, dx=k)))

    def owners_y():
        sy[0:2], sy[2:4] = joined("y", 0, lambda h: sum_ref[data_y(0, h, 0)])
        for j in (2, 1, 3, 0):
            for k in (2, 1, 3, 0):
                if (j, k) != (0, 0):
                    last.append(copies.start(sy.at[j, :, (px + k) % N], ry.at[j, k], device(dz=j, dx=k)))

    def relays(o):
        relay("x", o)
        relay("z", o)

    lax.fori_loop(0, 3, bricks(lambda i: i - 1), 0)
    pl.semaphore_wait(barrier, 1 + len(lines))
    for peer in lines:
        pl.semaphore_signal(ready_sem, inc=1, device_id=peer, device_id_type=MESH)
    send_pair(2)
    lax.fori_loop(3, 5, bricks(lambda i: i - 1), 0)
    send_pair(3)
    combine(2)
    lax.fori_loop(5, 7, bricks(lambda i: 8 - i), 0)
    send_pair(1)
    relays(2)
    combine(3)
    lax.fori_loop(7, 8, bricks(lambda i: i - 5), 0)
    send_pair(0)
    combine(1)
    relays(3)
    pl.semaphore_wait(ready_sem, len(lines))
    owners(2)
    combine(0)
    relays(1)
    owners(3)
    owners_y()
    relays(0)
    owners(1)
    owners(0)
    for copy in last:
        copy.wait_recv()

    def total(own, r):
        for j in range(N):
            for k in range(N):
                if (j, k) != (0, 0):
                    own = own + r[j, k]
        return own

    planes = jnp.concatenate([total(sx[0, 0], rx), total(sy[0, :, px], ry), total(sz[0, :, px], rz)], 0)
    rhs_ref[...] = planes[:BX]
    screen_ref[...] = planes[BX:]
    copies.finish()


def splat(first, q, start):
    vm = pl.BlockSpec(memory_space=pltpu.VMEM)
    f32 = jnp.float32
    nx, ny, nz = PARTS
    tile = (BY, BZ)
    made = N * N + 2 * 6 * N + 6 + 45
    shapes = ([(N, 2, 2, nx) + tile] * 4 + [(1, 2, 2, ny, N) + tile] * 4 + [(N, 2, nz, 2) + tile] * 4
              + [(N, N, nx) + tile, (N, ny, N) + tile, (N, nz, N) + tile]
              + [(N, N, nx) + tile, (N, N, ny) + tile, (N, N, nz) + tile])
    return pl.pallas_call(
        splat_kernel,
        out_shape=[jax.ShapeDtypeStruct((BX, BY, BZ), f32)] * 2,
        in_specs=[pl.BlockSpec(memory_space=pltpu.SMEM), vm, vm],
        out_specs=[vm, vm],
        scratch_shapes=[
            pltpu.VMEM((2 * PX * PY, BZ), f32),
            pltpu.VMEM((N, N, 2, BX, N * BY, BZ), f32),
            pltpu.VMEM((N, N, 2 * BX, N) + tile, f32),
            *[pltpu.VMEM(shape, f32) for shape in shapes],
            pltpu.SemaphoreType.DMA((made,)),
            pltpu.SemaphoreType.DMA((made,)),
            pltpu.SemaphoreType.REGULAR,
        ],
        compiler_params=pltpu.CompilerParams(collective_id=0, has_side_effects=True, vmem_limit_bytes=28 << 20),
        name="splat",
    )(first, q, start)


def shards(brick_ids, voxel_offset, fractions, normals, point_weight, tile_count):
    grid, q, first = prepare(brick_ids[:, 0], tile_count, voxel_offset, fractions, normals, point_weight)
    return tuple(splat(first, q, grid))


def solution(mesh):
    return jax.shard_map(
        shards,
        mesh=mesh,
        in_specs=(
            P(("gx", "yz"), None),
            P(("gx", "yz"), None),
            P(("gx", "yz"), None, None),
            P(("gx", "yz"), None, None),
            P(("gx", "yz"), None),
            P(("gx", "yz")),
        ),
        out_specs=(P("gx", "yz", None), P("gx", "yz", None)),
        check_vma=False,
    )
```

time: 44.8 us -> 39.3 us (0.88)
  local copies, waits for them, and re-layouts: 5.66 us -> 1.21 us
  Pallas kernels: 37.6 us -> 36.3 us
    unnamed x12 -> x2, local copies, waits for them, and re-layouts: 5.66 us -> 1.21 us
    pallas_call x1, Pallas kernels: 34.1 us -> 32.5 us  [splat(): pl.pallas_call(splat_kernel, out_shape=[jax.ShapeDtypeStruct((BX, BY, BZ)...]
where the time goes in v4:
time: 39.3 us; the launch traced here: 38.8 us
  Pallas kernels  36.3 us (92%)
  between operations  1.29 us (3%)
  local copies, waits for them, and re-layouts  1.21 us (3%)
    pallas_call x1, Pallas kernels, splat(): pl.pallas_call(splat_kernel, out_shape=[jax.ShapeDtypeStruct((BX, BY, BZ)...  32.5 us
    pallas_call x1, Pallas kernels, prepare(): pl.pallas_call(prepare_kernel, out_shape=[jax.ShapeDtypeStruct((2 * PX *...  3.86 us
    unnamed x2, local copies, waits for them, and re-layouts  1.21 us

profile of v4, /device:TPU:0, one launch (start us, length us, event | category | flops | bytes accessed | tf_op | source)
XLA Modules:
  0.0 38.8 jit_solution(6870529667268684709)
XLA Ops:
  1.3 3.9 %prepare.1 = (f32[10944,128]{1,0:T(8,128)S(1)}, f32[15872,128]{1,0:T(8,128)S(1)}, s32[128]{0:T(128)S(1)}) custom-call(s32[1]{0:T(128)S(6)} %copy.10.count_ref, s32[128]{0:T(128)} %bitcast.5, s32[128,256]{1,0:T(8,128)} %off_hbm.1, f32[3,128,256]{2,1,0:T(8,128)} %bitcast.3, f32[3,128,256]{2,1,0:T(8,128)} %bitcast.4, f32[128,256]{1,0:T(8,128)} %s_hbm.1), custom_call_target="tpu_custom_call" | custom-call | tf_op jit(solution)/shard_map/prepare/pallas_call | solution.py:189
  5.1 32.5 %splat.1 = (f32[4,8,128]{2,1,0:T(8,128)S(1)}, f32[4,8,128]{2,1,0:T(8,128)S(1)}) custom-call(s32[128]{0:T(128)S(1)} %get-tuple-element.5.first_ref, f32[15872,128]{1,0:T(8,128)S(1)} %get-tuple-element.6.q_ref, f32[10944,128]{1,0:T(8,128)S(1)} %get-tuple-element.7.start_ref), custom_call_target="tpu_custom_call" | custom-call | tf_op jit(solution)/shard_map/splat/pallas_call | solution.py:412
  37.6 0.6 %copy.11 = f32[4,8,128]{2,1,0:T(8,128)} copy(f32[4,8,128]{2,1,0:T(8,128)S(1)} %get-tuple-element.10) | data formatting | bytes 32768
  38.2 0.6 %copy.12 = f32[4,8,128]{2,1,0:T(8,128)} copy(f32[4,8,128]{2,1,0:T(8,128)S(1)} %get-tuple-element.11) | data formatting | bytes 32768

commit v5 on v4

--- a/solution.py
+++ b/solution.py
@@ -210,27 +210,33 @@
 class Copies:
     def __init__(self, send_sems, recv_sems):
         self.send_sems, self.recv_sems = send_sems, recv_sems
-        self.made = []
-
-    def start(self, src, dst, device):
-        i = len(self.made)
-        copy = pltpu.make_async_remote_copy(
+        self.made = {}
+
+    def start(self, key, where):
+        self.made[key] = (len(self.made), where)
+        self.copy(key).start()
+
+    def copy(self, key):
+        i, where = self.made[key]
+        src, dst, device = where()
+        return pltpu.make_async_remote_copy(
             src_ref=src, dst_ref=dst, send_sem=self.send_sems.at[i], recv_sem=self.recv_sems.at[i],
             device_id=device, device_id_type=MESH)
-        copy.start()
-        self.made.append(copy)
-        return copy
+
+    def arrived(self, key):
+        self.copy(key).wait_recv()
 
     def finish(self):
-        for copy in self.made:
-            copy.wait_send()
-
-
+        for key in self.made:
+            self.copy(key).wait_send()
+
+
+DIRECT = (0,)
 PARTS = (3, 3, 2)
 
 
 def splat_kernel(first_ref, q_ref, start_ref, rhs_ref, screen_ref, grid_ref, pair_ref, sum_ref,
-                 xa, xb, xc, xr, ya, yb, yc, yr, za, zb, zc, zr, sx, sy, sz, rx, ry, rz, send_sems, recv_sems, ready_sem):
+                 xa, xb, xc, xr, ya, yb, yc, yr, za, zb, zc, zr, xd, zd, sx, sy, sz, rx, ry, rz, send_sems, recv_sems, ready_sem):
     slab, column = lax.axis_index("gx"), lax.axis_index("yz")
     pz, core = slab // 2, slab % 2
     py, px = column // N, column % N
@@ -251,20 +257,8 @@
 
     lax.fori_loop(0, 2 * PX * PY // 96, fetch, 0)
 
-    def bricks(place):
-        def step(i, _):
-            ys = [(N * py + 2 * N + N * N + place(2 * i + k)) % (N * N) for k in range(2)]
-            places = [(x, y) for y in ys for x in range(2 * N)]
-            sums = [contract(*tile_build(first_ref[x * 16 + y], q_ref)) for x, y in places]
-            for (x, y), each in zip(places, sums):
-                add_in(x, y, each, grid_ref)
-            return 0
-        return step
-
     copies = Copies(send_sems, recv_sems)
     grid = grid_ref.reshape(2, PX, PY, BZ)
-    pair = {}
-
     def rows_of(o):
         return pl.ds(pl.multiple_of(BY + N * BY * ((py + o) % N), BY), N * BY)
 
@@ -273,57 +267,78 @@
 
     def send_pair(o):
         for j in range(N):
-            pair[o, j] = copies.start(grid.at[:, pl.ds(cells_of(j, 1 - core), BX), rows_of(o), :], pair_ref.at[o, j], other)
+            copies.start(("pair", o, j), lambda j=j: (
+                grid.at[:, pl.ds(cells_of(j, 1 - core), BX), rows_of(o), :], pair_ref.at[o, j], other))
 
     nx, ny, nz = PARTS
     xs, ys, zs = slice(0, nx), slice(nx, nx + ny), slice(nx + ny, nx + ny + nz)
 
-    def data_x(o, h, d):
-        return (o, slice(2 * h, 2 * h + 2), xs, (px + d) % N)
-
-    def data_y(o, h, d):
-        return (d % N, slice(2 * h, 2 * h + 2), ys)
-
-    def data_z(o, h, d):
-        return (o, d % N, zs, slice(2 * h, 2 * h + 2))
-
-    parts = {"x": (data_x, "dx", xa, xb, xc, xr), "y": (data_y, "dy", ya, yb, yc, yr), "z": (data_z, "dz", za, zb, zc, zr)}
-    first, second, third = {}, {}, {}
+    def half_of(h):
+        return slice(0, N) if h == 2 else slice(2 * h, 2 * h + 2)
+
+    def data(name, o, h, d):
+        if name == "x":
+            return (o, half_of(h), xs, (px + d) % N)
+        if name == "y":
+            return (d % N, half_of(h), ys)
+        return (o, d % N, zs, half_of(h))
+
+    buffers = {"x": (xa, xb, xc, xr), "y": (ya, yb, yc, yr), "z": (za, zb, zc, zr)}
+    straight = {"x": xd, "z": zd}
+
+    def along(name, d):
+        return device(**{"d" + name: d})
 
     def toward(name, way):
-        return device(**{parts[name][1]: 1 if way == 0 else N - 1})
+        return along(name, 1 if way == 0 else N - 1)
 
     def send_far(name, o):
-        data, _, a, _, _, _ = parts[name]
         for way in range(2):
-            first[name, o, way] = copies.start(sum_ref.at[data(o, way, 2)], a.at[o, way], toward(name, way))
+            copies.start(("a", name, o, way), lambda way=way: (
+                sum_ref.at[data(name, o, way, 2)], buffers[name][0].at[o, way], toward(name, way)))
 
     def send_near(name, o, ways=(0, 1)):
-        data, _, _, b, _, _ = parts[name]
         for way in ways:
-            second[name, o, way] = copies.start(sum_ref.at[data(o, 1 - way, 1 if way == 0 else N - 1)], b.at[o, way],
-                                                toward(name, way))
+            copies.start(("b", name, o, way), lambda way=way: (
+                sum_ref.at[data(name, o, 1 - way, 1 if way == 0 else N - 1)], buffers[name][1].at[o, way],
+                toward(name, way)))
 
     def relay(name, o, ways=(0, 1)):
-        data, _, a, _, c, r = parts[name]
+        a, _, _, r = buffers[name]
         for way in ways:
-            first[name, o, way].wait_recv()
-            r[o, way] = a[o, way] + sum_ref[data(o, way, 1 if way == 0 else N - 1)]
-            third[name, o, way] = copies.start(r.at[o, way], c.at[o, way], toward(name, way))
+            copies.arrived(("a", name, o, way))
+            r[o, way] = a[o, way] + sum_ref[data(name, o, way, 1 if way == 0 else N - 1)]
+            copies.start(("c", name, o, way), lambda way=way: (
+                buffers[name][3].at[o, way], buffers[name][2].at[o, way], toward(name, way)))
+
+    def send_straight(name, o):
+        for d in (2, 1, 3):
+            copies.start(("d", name, o, d), lambda d=d: (
+                sum_ref.at[data(name, o, 2, d)], straight[name].at[DIRECT.index(o), d - 1], along(name, d)))
 
     def combine(o):
         for j in range(N):
-            pair[o, j].wait_recv()
+            copies.arrived(("pair", o, j))
+
+        def add(j, _):
             for f in range(2):
                 for x in range(BX):
                     total = grid[f, cells_of(j, core) + x, rows_of(o), :] + pair_ref[o, j, f, x]
                     sum_ref[o, j, BX * f + x] = total.reshape(N, BY, BZ)
-        send_far("x", o)
-        send_far("z", o)
+            return 0
+
+        lax.fori_loop(0, N, add, 0)
+        if o in DIRECT:
+            send_straight("x", o)
+            send_straight("z", o)
+        else:
+            send_far("x", o)
+            send_far("z", o)
         if o == 2:
             send_far("y", 0)
-        send_near("x", o)
-        send_near("z", o)
+        if o not in DIRECT:
+            send_near("x", o)
+            send_near("z", o)
         if o == 3:
             relay("y", 0, (1,))
             send_near("y", 0, (1,))
@@ -331,47 +346,92 @@
             relay("y", 0, (0,))
             send_near("y", 0, (0,))
 
-    def joined(name, o, own):
-        _, _, _, b, c, _ = parts[name]
-        for way in range(2):
-            second[name, o, way].wait_recv()
-            third[name, o, way].wait_recv()
-        return [own(h) + c[o, h] + b[o, 1 - h] for h in range(2)]
+    def joined(name, o, h):
+        if o in DIRECT and name != "y":
+            half = (half_of(h),) if name == "x" else (slice(None), half_of(h))
+            total = sum_ref[data(name, o, h, 0)]
+            for d in range(1, N):
+                total = total + straight[name][(DIRECT.index(o), d - 1) + half]
+            return total
+        _, b, c, _ = buffers[name]
+        return sum_ref[data(name, o, h, 0)] + c[o, h] + b[o, 1 - h]
+
+    def settle(name, o):
+        if o in DIRECT and name != "y":
+            for d in range(1, N):
+                copies.arrived(("d", name, o, d))
+        else:
+            for way in range(2):
+                copies.arrived(("b", name, o, way))
+                copies.arrived(("c", name, o, way))
 
     last = []
 
+    def start_last(key, where):
+        copies.start(key, where)
+        last.append(key)
+
     def owners(o):
-        sx[o, 0:2], sx[o, 2:4] = joined("x", o, lambda h: sum_ref[data_x(o, h, 0)])
-        sz[o, :, 0:2], sz[o, :, 2:4] = joined("z", o, lambda h: sum_ref[data_z(o, h, 0)])
-        for k in (2, 1, 3, 0):
-            if (o, k) != (0, 0):
-                last.append(copies.start(sx.at[o, k], rx.at[o, k], device(dy=o, dz=k)))
-                last.append(copies.start(sz.at[o, :, (px + k) % N], rz.at[o, k], device(dy=o, dx=k)))
+        for name, s in (("x", sx), ("z", sz)):
+            settle(name, o)
+            for h in range(2):
+                if name == "x":
+                    s[o, half_of(h)] = joined(name, o, h)
+                else:
+                    s[o, :, half_of(h)] = joined(name, o, h)
+            for k in (2, 1, 3, 0):
+                if (o, k) != (0, 0):
+                    if name == "x":
+                        start_last(("last x", o, k), lambda k=k: (sx.at[o, k], rx.at[o, k], device(dy=o, dz=k)))
+                    else:
+                        start_last(("last z", o, k), lambda k=k: (sz.at[o, :, (px + k) % N], rz.at[o, k], device(dy=o, dx=k)))
 
     def owners_y():
-        sy[0:2], sy[2:4] = joined("y", 0, lambda h: sum_ref[data_y(0, h, 0)])
+        settle("y", 0)
+        for h in range(2):
+            sy[half_of(h)] = joined("y", 0, h)
         for j in (2, 1, 3, 0):
             for k in (2, 1, 3, 0):
                 if (j, k) != (0, 0):
-                    last.append(copies.start(sy.at[j, :, (px + k) % N], ry.at[j, k], device(dz=j, dx=k)))
+                    start_last(("last y", j, k), lambda j=j, k=k: (sy.at[j, :, (px + k) % N], ry.at[j, k], device(dz=j, dx=k)))
 
     def relays(o):
-        relay("x", o)
-        relay("z", o)
-
-    lax.fori_loop(0, 3, bricks(lambda i: i - 1), 0)
-    pl.semaphore_wait(barrier, 1 + len(lines))
-    for peer in lines:
-        pl.semaphore_signal(ready_sem, inc=1, device_id=peer, device_id_type=MESH)
-    send_pair(2)
-    lax.fori_loop(3, 5, bricks(lambda i: i - 1), 0)
-    send_pair(3)
-    combine(2)
-    lax.fori_loop(5, 7, bricks(lambda i: 8 - i), 0)
-    send_pair(1)
-    relays(2)
-    combine(3)
-    lax.fori_loop(7, 8, bricks(lambda i: i - 5), 0)
+        if o not in DIRECT:
+            relay("x", o)
+            relay("z", o)
+
+    def bricks(i, _):
+        ys = []
+        for k in range(2):
+            at = 2 * i + k
+            late, latest = at // 10, at // 14
+            place = (1 - late) * (at - 1) + (late - latest) * (8 - at) + latest * (at - 5)
+            ys.append((N * py + 2 * N + N * N + place) % (N * N))
+        places = [(x, y) for y in ys for x in range(2 * N)]
+        sums = [contract(*tile_build(first_ref[x * 16 + y], q_ref)) for x, y in places]
+        for (x, y), each in zip(places, sums):
+            add_in(x, y, each, grid_ref)
+
+        @pl.when(i == 2)
+        def _():
+            pl.semaphore_wait(barrier, 1 + len(lines))
+            for peer in lines:
+                pl.semaphore_signal(ready_sem, inc=1, device_id=peer, device_id_type=MESH)
+            send_pair(2)
+
+        @pl.when(i == 4)
+        def _():
+            send_pair(3)
+            combine(2)
+
+        @pl.when(i == 6)
+        def _():
+            send_pair(1)
+            relays(2)
+            combine(3)
+        return 0
+
+    lax.fori_loop(0, 8, bricks, 0)
     send_pair(0)
     combine(1)
     relays(3)
@@ -384,8 +444,8 @@
     relays(0)
     owners(1)
     owners(0)
-    for copy in last:
-        copy.wait_recv()
+    for key in last:
+        copies.arrived(key)
 
     def total(own, r):
         for j in range(N):
@@ -406,7 +466,9 @@
     nx, ny, nz = PARTS
     tile = (BY, BZ)
     made = N * N + 2 * 6 * N + 6 + 45
+    straight = max(1, len(DIRECT))
     shapes = ([(N, 2, 2, nx) + tile] * 4 + [(1, 2, 2, ny, N) + tile] * 4 + [(N, 2, nz, 2) + tile] * 4
+              + [(straight, N - 1, N, nx) + tile, (straight, N - 1, nz, N) + tile]
               + [(N, N, nx) + tile, (N, ny, N) + tile, (N, nz, N) + tile]
               + [(N, N, nx) + tile, (N, N, ny) + tile, (N, N, nz) + tile])
     return pl.pallas_call(

time: 39.3 us -> 37.2 us (0.947); the launches traced: 38.8 us -> 37.2 us
  Pallas kernels: 36.3 us -> 34.7 us
    pallas_call x1, Pallas kernels: 32.5 us -> 30.8 us  [splat(): pl.pallas_call(splat_kernel, out_shape=[jax.ShapeDtypeStruct((BX, BY, BZ)...]
where the time goes in v5:
time: 37.2 us
  Pallas kernels  34.7 us (93%)
  between operations  1.29 us (3%)
  local copies, waits for them, and re-layouts  1.21 us (3%)
    pallas_call x1, Pallas kernels, splat(): pl.pallas_call(splat_kernel, out_shape=[jax.ShapeDtypeStruct((BX, BY, BZ)...  30.8 us
    pallas_call x1, Pallas kernels, prepare(): pl.pallas_call(prepare_kernel, out_shape=[jax.ShapeDtypeStruct((2 * PX *...  3.85 us
    unnamed x2, local copies, waits for them, and re-layouts  1.21 us

profile of v5, /device:TPU:0, one launch (start us, length us, event | category | flops | bytes accessed | tf_op | source)
XLA Modules:
  0.0 37.2 jit_solution(5267438441569671701)
XLA Ops:
  1.3 3.9 %prepare.1 = (f32[10944,128]{1,0:T(8,128)S(1)}, f32[15872,128]{1,0:T(8,128)S(1)}, s32[128]{0:T(128)S(1)}) custom-call(s32[1]{0:T(128)S(6)} %copy.10.count_ref, s32[128]{0:T(128)} %bitcast.5, s32[128,256]{1,0:T(8,128)} %off_hbm.1, f32[3,128,256]{2,1,0:T(8,128)} %bitcast.3, f32[3,128,256]{2,1,0:T(8,128)} %bitcast.4, f32[128,256]{1,0:T(8,128)} %s_hbm.1), custom_call_target="tpu_custom_call" | custom-call | tf_op jit(solution)/shard_map/prepare/pallas_call | solution.py:189
  5.1 30.8 %splat.1 = (f32[4,8,128]{2,1,0:T(8,128)S(1)}, f32[4,8,128]{2,1,0:T(8,128)S(1)}) custom-call(s32[128]{0:T(128)S(1)} %get-tuple-element.5.first_ref, f32[15872,128]{1,0:T(8,128)S(1)} %get-tuple-element.6.q_ref, f32[10944,128]{1,0:T(8,128)S(1)} %get-tuple-element.7.start_ref), custom_call_target="tpu_custom_call" | custom-call | tf_op jit(solution)/shard_map/splat/pallas_call | solution.py:474
  36.0 0.6 %copy.11 = f32[4,8,128]{2,1,0:T(8,128)} copy(f32[4,8,128]{2,1,0:T(8,128)S(1)} %get-tuple-element.10) | data formatting | bytes 32768
  36.6 0.6 %copy.12 = f32[4,8,128]{2,1,0:T(8,128)} copy(f32[4,8,128]{2,1,0:T(8,128)S(1)} %get-tuple-element.11) | data formatting | bytes 32768

commit v6 on v5

--- a/solution.py
+++ b/solution.py
@@ -101,8 +101,8 @@
             out_ref[r, :] += res[f][48 + 8 * k:56 + 8 * k]
 
 
-def prepare_kernel(count_ref, dest_hbm, off_hbm, frac_hbm, norm_hbm, s_hbm, grid_ref, q_ref, first_ref,
-                   dest_ref, off_ref, frac_ref, norm_ref, s_ref, list_ref, sems):
+def prepare_kernel(count_ref, dest_hbm, off_hbm, frac_hbm, norm_hbm, s_hbm, grid_ref, q_ref, first_out,
+                   dest_ref, off_ref, frac_ref, norm_ref, s_ref, list_ref, first_ref, sems):
     pairs = ((dest_hbm, dest_ref), (off_hbm, off_ref), (frac_hbm, frac_ref), (norm_hbm, norm_ref),
              (s_hbm, s_ref))
     loads = [pltpu.make_async_copy(src, dst, sems.at[i]) for i, (src, dst) in enumerate(pairs)]
@@ -168,6 +168,8 @@
         return seconds
 
     seconds = lax.fori_loop(0, NONE // 8, group, 0)
+    table = pltpu.make_async_copy(first_ref, first_out, sems.at[5])
+    table.start()
     for k in range(V):
         list_ref[seconds + k] = NONE
 
@@ -180,6 +182,7 @@
         return 0
 
     lax.fori_loop(0, (seconds + V - 1) // V, more, 0)
+    table.wait()
 
 
 def prepare(dest, count, off, frac, norm, s):
@@ -191,11 +194,11 @@
         out_shape=[jax.ShapeDtypeStruct((2 * PX * PY, BZ), f32), jax.ShapeDtypeStruct((NONE * ROWS + 128, 128), f32),
                    jax.ShapeDtypeStruct((tiles,), jnp.int32)],
         in_specs=[pl.BlockSpec(memory_space=pltpu.SMEM)] + [hbm] * 5,
-        out_specs=[pl.BlockSpec(memory_space=pltpu.VMEM)] * 2 + [pl.BlockSpec(memory_space=pltpu.SMEM)],
+        out_specs=[pl.BlockSpec(memory_space=pltpu.VMEM)] * 2 + [pl.BlockSpec(memory_space=pl.ANY)],
         scratch_shapes=[
             pltpu.SMEM((tiles,), jnp.int32), pltpu.VMEM((tiles, n), jnp.int32),
             pltpu.VMEM((3, tiles, n), f32), pltpu.VMEM((3, tiles, n), f32), pltpu.VMEM((tiles, n), f32),
-            pltpu.SMEM((tiles + 2 * V,), jnp.int32), pltpu.SemaphoreType.DMA((5,)),
+            pltpu.SMEM((tiles + 2 * V,), jnp.int32), pltpu.SMEM((tiles,), jnp.int32), pltpu.SemaphoreType.DMA((6,)),
         ],
         compiler_params=pltpu.CompilerParams(vmem_limit_bytes=22 << 20),
         name="prepare",
@@ -231,12 +234,12 @@
             self.copy(key).wait_send()
 
 
-DIRECT = (0,)
-PARTS = (3, 3, 2)
-
-
-def splat_kernel(first_ref, q_ref, start_ref, rhs_ref, screen_ref, grid_ref, pair_ref, sum_ref,
-                 xa, xb, xc, xr, ya, yb, yc, yr, za, zb, zc, zr, xd, zd, sx, sy, sz, rx, ry, rz, send_sems, recv_sems, ready_sem):
+DIRECT = (0, 1, 3)
+PARTS = (3, 2, 3)
+
+
+def splat_kernel(first_hbm, q_ref, start_ref, out_ref, grid_ref, pair_ref, sum_ref,
+                 xa, xb, xc, xr, ya, yb, yc, yr, za, zb, zc, zr, xd, zd, sx, sy, sz, rx, ry, rz, send_sems, recv_sems, ready_sem, first_ref, table_sem):
     slab, column = lax.axis_index("gx"), lax.axis_index("yz")
     pz, core = slab // 2, slab % 2
     py, px = column // N, column % N
@@ -250,12 +253,20 @@
     for peer in [other] + lines:
         pl.semaphore_signal(barrier, inc=1, device_id=peer, device_id_type=MESH)
 
-    def fetch(i, _):
-        r = pl.ds(pl.multiple_of(i * 96, 96), 96)
-        grid_ref[r, :] = start_ref[r, :]
+    table = pltpu.make_async_copy(first_hbm, first_ref, table_sem)
+    table.start()
+
+    def fetch(y):
+        for row in range(2 * PX):
+            r = pl.ds(pl.multiple_of(row * PY + BY + BY * y, BY), BY)
+            grid_ref[r, :] = start_ref[r, :]
+
+    def fetch_first(k, _):
+        fetch((N * py + 2 * N + N * N - 2 + k) % (N * N))
         return 0
 
-    lax.fori_loop(0, 2 * PX * PY // 96, fetch, 0)
+    lax.fori_loop(0, 4, fetch_first, 0)
+    table.wait()
 
     copies = Copies(send_sems, recv_sems)
     grid = grid_ref.reshape(2, PX, PY, BZ)
@@ -401,6 +412,10 @@
             relay("z", o)
 
     def bricks(i, _):
+        back, done = i // 4, i // 6
+        for k in range(2):
+            place = (1 - back) * (2 + 2 * i) + back * (4 - 2 * i) + k
+            fetch((1 - done) * ((N * py + 2 * N + N * N + place) % (N * N)) + done * N * N)
         ys = []
         for k in range(2):
             at = 2 * i + k
@@ -455,8 +470,7 @@
         return own
 
     planes = jnp.concatenate([total(sx[0, 0], rx), total(sy[0, :, px], ry), total(sz[0, :, px], rz)], 0)
-    rhs_ref[...] = planes[:BX]
-    screen_ref[...] = planes[BX:]
+    out_ref[...] = planes
     copies.finish()
 
 
@@ -473,9 +487,9 @@
               + [(N, N, nx) + tile, (N, N, ny) + tile, (N, N, nz) + tile])
     return pl.pallas_call(
         splat_kernel,
-        out_shape=[jax.ShapeDtypeStruct((BX, BY, BZ), f32)] * 2,
-        in_specs=[pl.BlockSpec(memory_space=pltpu.SMEM), vm, vm],
-        out_specs=[vm, vm],
+        out_shape=jax.ShapeDtypeStruct((2 * BX, BY, BZ), f32),
+        in_specs=[pl.BlockSpec(memory_space=pl.ANY), vm, vm],
+        out_specs=vm,
         scratch_shapes=[
             pltpu.VMEM((2 * PX * PY, BZ), f32),
             pltpu.VMEM((N, N, 2, BX, N * BY, BZ), f32),
@@ -484,15 +498,38 @@
             pltpu.SemaphoreType.DMA((made,)),
             pltpu.SemaphoreType.DMA((made,)),
             pltpu.SemaphoreType.REGULAR,
+            pltpu.SMEM((NONE,), jnp.int32),
+            pltpu.SemaphoreType.DMA,
         ],
         compiler_params=pltpu.CompilerParams(collective_id=0, has_side_effects=True, vmem_limit_bytes=28 << 20),
         name="splat",
     )(first, q, start)
 
 
+def part_kernel(planes_ref, rhs_hbm, screen_hbm, sems):
+    copies = [pltpu.make_async_copy(planes_ref.at[pl.ds(BX * i, BX)], hbm, sems.at[i])
+              for i, hbm in enumerate((rhs_hbm, screen_hbm))]
+    for copy in copies:
+        copy.start()
+    for copy in copies:
+        copy.wait()
+
+
+def part(planes):
+    hbm = pl.BlockSpec(memory_space=pltpu.HBM)
+    return pl.pallas_call(
+        part_kernel,
+        out_shape=[jax.ShapeDtypeStruct((BX, BY, BZ), jnp.float32)] * 2,
+        in_specs=[pl.BlockSpec(memory_space=pltpu.VMEM)],
+        out_specs=[hbm, hbm],
+        scratch_shapes=[pltpu.SemaphoreType.DMA((2,))],
+        name="part",
+    )(planes)
+
+
 def shards(brick_ids, voxel_offset, fractions, normals, point_weight, tile_count):
     grid, q, first = prepare(brick_ids[:, 0], tile_count, voxel_offset, fractions, normals, point_weight)
-    return tuple(splat(first, q, grid))
+    return tuple(part(pltpu.with_memory_space_constraint(splat(first, q, grid), pltpu.VMEM)))
 
 
 def solution(mesh):

time: 37.2 us -> 35.9 us (0.965)
  local copies, waits for them, and re-layouts: 1.21 us -> 0 us
    unnamed x2 -> x0, local copies, waits for them, and re-layouts: 1.21 us -> none
    pallas_call x1 -> x2, Pallas kernels: 30.8 us -> 31.5 us  [the longest x1 30.9 us: splat(): pl.pallas_call(splat_kernel, out_shape=jax.ShapeDtypeStruct((2 * BX, BY,...]
    pallas_call x1, Pallas kernels: 3.85 us -> 3.27 us  [prepare(): pl.pallas_call(prepare_kernel, out_shape=[jax.ShapeDtypeStruct((2 * PX *...]
where the time goes in v6:
time: 35.9 us; the launch traced here: 36.1 us
  Pallas kernels  34.8 us (97%)
  between operations  1.29 us (4%)
    pallas_call x1, Pallas kernels, splat(): pl.pallas_call(splat_kernel, out_shape=jax.ShapeDtypeStruct((2 * BX, BY,...  30.9 us
    pallas_call x1, Pallas kernels, prepare(): pl.pallas_call(prepare_kernel, out_shape=[jax.ShapeDtypeStruct((2 * PX *...  3.27 us

profile of v6, /device:TPU:0, one launch (start us, length us, event | category | flops | bytes accessed | tf_op | source)
XLA Modules:
  0.0 36.1 jit_solution(4378947849403254670)
XLA Ops:
  1.3 3.3 %prepare.1 = (f32[10944,128]{1,0:T(8,128)S(1)}, f32[15872,128]{1,0:T(8,128)S(1)}, s32[128]{0:T(128)S(1)}) custom-call(s32[1]{0:T(128)S(6)} %copy.8.count_ref, s32[128]{0:T(128)} %bitcast.5, s32[128,256]{1,0:T(8,128)} %off_hbm.1, f32[3,128,256]{2,1,0:T(8,128)} %bitcast.3, f32[3,128,256]{2,1,0:T(8,128)} %bitcast.4, f32[128,256]{1,0:T(8,128)} %s_hbm.1), custom_call_target="tpu_custom_call" | custom-call | tf_op jit(solution)/shard_map/prepare/pallas_call | solution.py:192
  4.6 30.9 %splat.1.planes_ref = f32[8,8,128]{2,1,0:T(8,128)S(1)} custom-call(s32[128]{0:T(128)S(1)} %get-tuple-element.5.first_hbm, f32[15872,128]{1,0:T(8,128)S(1)} %get-tuple-element.6.q_ref, f32[10944,128]{1,0:T(8,128)S(1)} %get-tuple-element.7.start_ref), custom_call_target="tpu_custom_call" | custom-call | tf_op jit(solution)/shard_map/splat/pallas_call | solution.py:488
  35.5 0.6 %part.1 = (f32[4,8,128]{2,1,0:T(8,128)}, f32[4,8,128]{2,1,0:T(8,128)}) custom-call(f32[8,8,128]{2,1,0:T(8,128)S(1)} %splat.1.planes_ref), custom_call_target="tpu_custom_call" | custom-call | tf_op jit(solution)/shard_map/part/pallas_call | solution.py:520

commit v7 on v6

--- a/solution.py
+++ b/solution.py
@@ -213,28 +213,40 @@
 class Copies:
     def __init__(self, send_sems, recv_sems):
         self.send_sems, self.recv_sems = send_sems, recv_sems
-        self.made = {}
+        self.made, self.used = {}, 0
 
     def start(self, key, where):
-        self.made[key] = (len(self.made), where)
-        self.copy(key).start()
-
-    def copy(self, key):
-        i, where = self.made[key]
-        src, dst, device = where()
-        return pltpu.make_async_remote_copy(
-            src_ref=src, dst_ref=dst, send_sem=self.send_sems.at[i], recv_sem=self.recv_sems.at[i],
-            device_id=device, device_id_type=MESH)
+        self.many(key, 1, lambda i: where())
+
+    def many(self, key, count, where):
+        self.made[key] = (self.used, count, where)
+        self.used += count
+        self.each(key, lambda copy: copy.start())
+
+    def each(self, key, act):
+        base, count, where = self.made[key]
+
+        def one(i, _):
+            src, dst, device = where(i)
+            act(pltpu.make_async_remote_copy(
+                src_ref=src, dst_ref=dst, send_sem=self.send_sems.at[base + i], recv_sem=self.recv_sems.at[base + i],
+                device_id=device, device_id_type=MESH))
+            return 0
+
+        if count == 1:
+            one(0, 0)
+        else:
+            lax.fori_loop(0, count, one, 0)
 
     def arrived(self, key):
-        self.copy(key).wait_recv()
+        self.each(key, lambda copy: copy.wait_recv())
 
     def finish(self):
         for key in self.made:
-            self.copy(key).wait_send()
-
-
-DIRECT = (0, 1, 3)
+            self.each(key, lambda copy: copy.wait_send())
+
+
+DIRECT = (0, 1, 2, 3)
 PARTS = (3, 2, 3)
 
 
@@ -277,9 +289,8 @@
         return 1 + BX * (((pz + j) % N) * 2 + which)
 
     def send_pair(o):
-        for j in range(N):
-            copies.start(("pair", o, j), lambda j=j: (
-                grid.at[:, pl.ds(cells_of(j, 1 - core), BX), rows_of(o), :], pair_ref.at[o, j], other))
+        copies.many(("pair", o), N, lambda j: (
+            grid.at[:, pl.ds(cells_of(j, 1 - core), BX), rows_of(o), :], pair_ref.at[o, j], other))
 
     nx, ny, nz = PARTS
     xs, ys, zs = slice(0, nx), slice(nx, nx + ny), slice(nx + ny, nx + ny + nz)
@@ -323,13 +334,14 @@
                 buffers[name][3].at[o, way], buffers[name][2].at[o, way], toward(name, way)))
 
     def send_straight(name, o):
-        for d in (2, 1, 3):
-            copies.start(("d", name, o, d), lambda d=d: (
-                sum_ref.at[data(name, o, 2, d)], straight[name].at[DIRECT.index(o), d - 1], along(name, d)))
+        def where(i):
+            d = (i + 1) % (N - 1) + 1
+            return sum_ref.at[data(name, o, 2, d)], straight[name].at[DIRECT.index(o), d - 1], along(name, d)
+
+        copies.many(("d", name, o), N - 1, where)
 
     def combine(o):
-        for j in range(N):
-            copies.arrived(("pair", o, j))
+        copies.arrived(("pair", o))
 
         def add(j, _):
             for f in range(2):
@@ -369,8 +381,7 @@
 
     def settle(name, o):
         if o in DIRECT and name != "y":
-            for d in range(1, N):
-                copies.arrived(("d", name, o, d))
+            copies.arrived(("d", name, o))
         else:
             for way in range(2):
                 copies.arrived(("b", name, o, way))
@@ -378,8 +389,8 @@
 
     last = []
 
-    def start_last(key, where):
-        copies.start(key, where)
+    def send_last(key, first, count, where):
+        copies.many(key, count - first, lambda i: where(i + first))
         last.append(key)
 
     def owners(o):
@@ -390,26 +401,19 @@
                     s[o, half_of(h)] = joined(name, o, h)
                 else:
                     s[o, :, half_of(h)] = joined(name, o, h)
-            for k in (2, 1, 3, 0):
-                if (o, k) != (0, 0):
-                    if name == "x":
-                        start_last(("last x", o, k), lambda k=k: (sx.at[o, k], rx.at[o, k], device(dy=o, dz=k)))
-                    else:
-                        start_last(("last z", o, k), lambda k=k: (sz.at[o, :, (px + k) % N], rz.at[o, k], device(dy=o, dx=k)))
+        send_last(("last x", o), int(o == 0), N, lambda k: (sx.at[o, k], rx.at[o, k], device(dy=o, dz=k)))
+        send_last(("last z", o), int(o == 0), N, lambda k: (sz.at[o, :, (px + k) % N], rz.at[o, k], device(dy=o, dx=k)))
 
     def owners_y():
         settle("y", 0)
         for h in range(2):
             sy[half_of(h)] = joined("y", 0, h)
-        for j in (2, 1, 3, 0):
-            for k in (2, 1, 3, 0):
-                if (j, k) != (0, 0):
-                    start_last(("last y", j, k), lambda j=j, k=k: (sy.at[j, :, (px + k) % N], ry.at[j, k], device(dz=j, dx=k)))
-
-    def relays(o):
-        if o not in DIRECT:
-            relay("x", o)
-            relay("z", o)
+
+        def where(i):
+            j, k = i // N, i % N
+            return sy.at[j, :, (px + k) % N], ry.at[j, k], device(dz=j, dx=k)
+
+        send_last("last y", 1, N * N, where)
 
     def bricks(i, _):
         back, done = i // 4, i // 6
@@ -442,21 +446,17 @@
         @pl.when(i == 6)
         def _():
             send_pair(1)
-            relays(2)
             combine(3)
         return 0
 
     lax.fori_loop(0, 8, bricks, 0)
     send_pair(0)
     combine(1)
-    relays(3)
     pl.semaphore_wait(ready_sem, len(lines))
+    combine(0)
     owners(2)
-    combine(0)
-    relays(1)
     owners(3)
     owners_y()
-    relays(0)
     owners(1)
     owners(0)
     for key in last:

time: 35.9 us -> 34 us (0.947)
  Pallas kernels: 34.8 us -> 32.6 us
    pallas_call x1, Pallas kernels: 30.9 us -> 29.1 us  [splat(): pl.pallas_call(splat_kernel, out_shape=jax.ShapeDtypeStruct((2 * BX, BY,...]
    pallas_call x1, Pallas kernels: 3.27 us -> 2.86 us  [prepare(): pl.pallas_call(prepare_kernel, out_shape=[jax.ShapeDtypeStruct((2 * PX *...]
where the time goes in v7:
time: 34 us; the launch traced here: 33.9 us
  Pallas kernels  32.6 us (96%)
  between operations  1.29 us (4%)
    pallas_call x1, Pallas kernels, splat(): pl.pallas_call(splat_kernel, out_shape=jax.ShapeDtypeStruct((2 * BX, BY,...  29.1 us
    pallas_call x1, Pallas kernels, prepare(): pl.pallas_call(prepare_kernel, out_shape=[jax.ShapeDtypeStruct((2 * PX *...  2.86 us

profile of v7, /device:TPU:0, one launch (start us, length us, event | category | flops | bytes accessed | tf_op | source)
XLA Modules:
  0.0 33.9 jit_solution(7365911944574063350)
XLA Ops:
  1.3 2.9 %prepare.1 = (f32[10944,128]{1,0:T(8,128)S(1)}, f32[15872,128]{1,0:T(8,128)S(1)}, s32[128]{0:T(128)S(1)}) custom-call(s32[1]{0:T(128)S(6)} %copy.8.count_ref, s32[128]{0:T(128)} %bitcast.5, s32[128,256]{1,0:T(8,128)} %off_hbm.1, f32[3,128,256]{2,1,0:T(8,128)} %bitcast.3, f32[3,128,256]{2,1,0:T(8,128)} %bitcast.4, f32[128,256]{1,0:T(8,128)} %s_hbm.1), custom_call_target="tpu_custom_call" | custom-call | tf_op jit(solution)/shard_map/prepare/pallas_call | solution.py:192
  4.1 29.1 %splat.1.planes_ref = f32[8,8,128]{2,1,0:T(8,128)S(1)} custom-call(s32[128]{0:T(128)S(1)} %get-tuple-element.5.first_hbm, f32[15872,128]{1,0:T(8,128)S(1)} %get-tuple-element.6.q_ref, f32[10944,128]{1,0:T(8,128)S(1)} %get-tuple-element.7.start_ref), custom_call_target="tpu_custom_call" | custom-call | tf_op jit(solution)/shard_map/splat/pallas_call | solution.py:488
  33.2 0.6 %part.1 = (f32[4,8,128]{2,1,0:T(8,128)}, f32[4,8,128]{2,1,0:T(8,128)}) custom-call(f32[8,8,128]{2,1,0:T(8,128)S(1)} %splat.1.planes_ref), custom_call_target="tpu_custom_call" | custom-call | tf_op jit(solution)/shard_map/part/pallas_call | solution.py:520

commit v8 on v7

--- a/solution.py
+++ b/solution.py
@@ -459,6 +459,7 @@
     owners_y()
     owners(1)
     owners(0)
+    copies.finish()
     for key in last:
         copies.arrived(key)
 
@@ -471,7 +472,6 @@
 
     planes = jnp.concatenate([total(sx[0, 0], rx), total(sy[0, :, px], ry), total(sz[0, :, px], rz)], 0)
     out_ref[...] = planes
-    copies.finish()
 
 
 def splat(first, q, start):

time: 34 us -> 33.4 us (0.982)
  Pallas kernels: 32.6 us -> 32 us
    pallas_call x1, Pallas kernels: 29.1 us -> 28.1 us  [splat(): pl.pallas_call(splat_kernel, out_shape=jax.ShapeDtypeStruct((2 * BX, BY,...]
    pallas_call x1, Pallas kernels: 2.86 us -> 3.28 us  [prepare(): pl.pallas_call(prepare_kernel, out_shape=[jax.ShapeDtypeStruct((2 * PX *...]
where the time goes in v8:
time: 33.4 us; the launch traced here: 33.3 us
  Pallas kernels  32 us (96%)
  between operations  1.29 us (4%)
    pallas_call x1, Pallas kernels, splat(): pl.pallas_call(splat_kernel, out_shape=jax.ShapeDtypeStruct((2 * BX, BY,...  28.1 us
    pallas_call x1, Pallas kernels, prepare(): pl.pallas_call(prepare_kernel, out_shape=[jax.ShapeDtypeStruct((2 * PX *...  3.28 us

profile of v8, /device:TPU:0, one launch (start us, length us, event | category | flops | bytes accessed | tf_op | source)
XLA Modules:
  0.0 33.3 jit_solution(8445888698703479196)
XLA Ops:
  1.3 3.3 %prepare.1 = (f32[10944,128]{1,0:T(8,128)S(1)}, f32[15872,128]{1,0:T(8,128)S(1)}, s32[128]{0:T(128)S(1)}) custom-call(s32[1]{0:T(128)S(6)} %copy.8.count_ref, s32[128]{0:T(128)} %bitcast.5, s32[128,256]{1,0:T(8,128)} %off_hbm.1, f32[3,128,256]{2,1,0:T(8,128)} %bitcast.3, f32[3,128,256]{2,1,0:T(8,128)} %bitcast.4, f32[128,256]{1,0:T(8,128)} %s_hbm.1), custom_call_target="tpu_custom_call" | custom-call | tf_op jit(solution)/shard_map/prepare/pallas_call | solution.py:192
  4.6 28.1 %splat.1.planes_ref = f32[8,8,128]{2,1,0:T(8,128)S(1)} custom-call(s32[128]{0:T(128)S(1)} %get-tuple-element.5.first_hbm, f32[15872,128]{1,0:T(8,128)S(1)} %get-tuple-element.6.q_ref, f32[10944,128]{1,0:T(8,128)S(1)} %get-tuple-element.7.start_ref), custom_call_target="tpu_custom_call" | custom-call | tf_op jit(solution)/shard_map/splat/pallas_call | solution.py:488
  32.6 0.6 %part.1 = (f32[4,8,128]{2,1,0:T(8,128)}, f32[4,8,128]{2,1,0:T(8,128)}) custom-call(f32[8,8,128]{2,1,0:T(8,128)S(1)} %splat.1.planes_ref), custom_call_target="tpu_custom_call" | custom-call | tf_op jit(solution)/shard_map/part/pallas_call | solution.py:520

commit v9 on v8

--- a/solution.py
+++ b/solution.py
@@ -389,8 +389,8 @@
 
     last = []
 
-    def send_last(key, first, count, where):
-        copies.many(key, count - first, lambda i: where(i + first))
+    def send_last(key, first, count, ahead, where):
+        copies.many(key, count - first, lambda i: where((i + ahead) % (count - first) + first))
         last.append(key)
 
     def owners(o):
@@ -401,8 +401,8 @@
                     s[o, half_of(h)] = joined(name, o, h)
                 else:
                     s[o, :, half_of(h)] = joined(name, o, h)
-        send_last(("last x", o), int(o == 0), N, lambda k: (sx.at[o, k], rx.at[o, k], device(dy=o, dz=k)))
-        send_last(("last z", o), int(o == 0), N, lambda k: (sz.at[o, :, (px + k) % N], rz.at[o, k], device(dy=o, dx=k)))
+        send_last(("last x", o), int(o == 0), N, 2 - int(o == 0), lambda k: (sx.at[o, k], rx.at[o, k], device(dy=o, dz=k)))
+        send_last(("last z", o), int(o == 0), N, 2 - int(o == 0), lambda k: (sz.at[o, :, (px + k) % N], rz.at[o, k], device(dy=o, dx=k)))
 
     def owners_y():
         settle("y", 0)
@@ -413,7 +413,7 @@
             j, k = i // N, i % N
             return sy.at[j, :, (px + k) % N], ry.at[j, k], device(dz=j, dx=k)
 
-        send_last("last y", 1, N * N, where)
+        send_last("last y", 1, N * N, 2 * N + 1, where)
 
     def bricks(i, _):
         back, done = i // 4, i // 6

time: 33.4 us -> 33.4 us (level)
  no operation moved by 1% of the time
where the time goes in v9:
time: 33.4 us; the launch traced here: 33.3 us
  Pallas kernels  32 us (96%)
  between operations  1.29 us (4%)
    pallas_call x1, Pallas kernels, splat(): pl.pallas_call(splat_kernel, out_shape=jax.ShapeDtypeStruct((2 * BX, BY,...  28.1 us
    pallas_call x1, Pallas kernels, prepare(): pl.pallas_call(prepare_kernel, out_shape=[jax.ShapeDtypeStruct((2 * PX *...  3.27 us

profile of v9, /device:TPU:0, one launch (start us, length us, event | category | flops | bytes accessed | tf_op | source)
XLA Modules:
  0.0 33.3 jit_solution(2834977077840254890)
XLA Ops:
  1.3 3.3 %prepare.1 = (f32[10944,128]{1,0:T(8,128)S(1)}, f32[15872,128]{1,0:T(8,128)S(1)}, s32[128]{0:T(128)S(1)}) custom-call(s32[1]{0:T(128)S(6)} %copy.8.count_ref, s32[128]{0:T(128)} %bitcast.5, s32[128,256]{1,0:T(8,128)} %off_hbm.1, f32[3,128,256]{2,1,0:T(8,128)} %bitcast.3, f32[3,128,256]{2,1,0:T(8,128)} %bitcast.4, f32[128,256]{1,0:T(8,128)} %s_hbm.1), custom_call_target="tpu_custom_call" | custom-call | tf_op jit(solution)/shard_map/prepare/pallas_call | solution.py:192
  4.6 28.1 %splat.1.planes_ref = f32[8,8,128]{2,1,0:T(8,128)S(1)} custom-call(s32[128]{0:T(128)S(1)} %get-tuple-element.5.first_hbm, f32[15872,128]{1,0:T(8,128)S(1)} %get-tuple-element.6.q_ref, f32[10944,128]{1,0:T(8,128)S(1)} %get-tuple-element.7.start_ref), custom_call_target="tpu_custom_call" | custom-call | tf_op jit(solution)/shard_map/splat/pallas_call | solution.py:488
  32.6 0.6 %part.1 = (f32[4,8,128]{2,1,0:T(8,128)}, f32[4,8,128]{2,1,0:T(8,128)}) custom-call(f32[8,8,128]{2,1,0:T(8,128)S(1)} %splat.1.planes_ref), custom_call_target="tpu_custom_call" | custom-call | tf_op jit(solution)/shard_map/part/pallas_call | solution.py:520
